TPU v7x, 32 devices: a whole 2x2x4 slice. The times are simulated.
32 devices in a mesh: row: 4 (over y, x), col: 8 (over z, core).
Axes of the slice: x: 2, y: 2, z: 4, core: 2. Of those that a mesh axis runs over, the one named last changes fastest.
Arguments:
- features: bfloat16 [131072, 256], P(('row', 'col')), may hold values from -6 to 6
- send_rows: int32 [32, 32, 128], P(('row', 'col')), may hold values from 0 to 4095
- counts: int32 [32, 32], P(('row', 'col')), may hold values from 112 to 128, as said below
- tile_dst: int32 [32, 64], P(('row', 'col')), may hold values from 0 to 31
- tile_src: int32 [32, 64], P(('row', 'col')), may hold values from 0 to 63, each once within a row
- tiles: int32 [32, 64, 128, 128], P(('row', 'col')), may hold values 0 or 1
- w_self: bfloat16 [256, 256], replicated, may hold values from -0.375 to 0.375
- w_neigh: bfloat16 [256, 256], replicated, may hold values from -1.5 to 1.5
- bias: float32 [256], replicated, may hold values from -1 to 1
- cotangent: bfloat16 [131072, 256], P(('row', 'col')), may hold values from -6 to 6
Outputs:
- layer_out: bfloat16 [131072, 256], P(('row', 'col'))
- grad_features: float32 [131072, 256], P(('row', 'col'))
- grad_self: float32 [256, 256], replicated
- grad_neigh: float32 [256, 256], replicated
- grad_bias: float32 [256], replicated
Inputs may be any that keep to these rules, and one draw needn't show every extreme that they name: Every partition p has some q with counts[p, q] = 128.
All inputs are finite; a program needn't handle non-finite values. No bound on the sum of `tiles` on one device may be relied on, other than what follows from the above.
Results may differ from a plain program's by a relative error of at most 0.0051.
Values may be sent and summed in bfloat16 or wider, within the bound.
No kernel may reach another device: no remote copies, remote signals or barrier semaphores. Data moves between devices by JAX's collectives and lax.ppermute only.
A program may use at most 192 MiB of HBM per device.

v0:
```python
import jax
import jax.numpy as jnp
from jax import lax
from jax.sharding import PartitionSpec as P


def move_rows(block):
    return lax.all_to_all(block, ("row", "col"), split_axis=0, concat_axis=0, tiled=True)


def move_grads(block):
    return lax.all_to_all(block, ("row", "col"), split_axis=0, concat_axis=0, tiled=True)


def on_device(
    features, send_rows, counts, tile_dst, tile_src, tiles, w_self, w_neigh, bias, cotangent
):
    rows_own, width = features.shape
    peers = send_rows.shape[1]
    tile_rows = send_rows.shape[2]
    own_blocks = rows_own // tile_rows
    src_blocks = own_blocks + peers
    picks = send_rows[0]
    slots = jnp.arange(tile_rows, dtype=jnp.int32)
    keep = (slots[None, :] < counts[0][:, None]).reshape(-1)
    flat_picks = picks.reshape(-1)
    outgoing = jnp.take(features, flat_picks, axis=0) * keep[:, None].astype(jnp.bfloat16)
    arrived = move_rows(outgoing.reshape(peers, tile_rows, width))
    source = jnp.concatenate([features, arrived.reshape(peers * tile_rows, width)], 0)
    source = source.reshape(src_blocks, tile_rows, width)
    dst = tile_dst[0]
    src = tile_src[0]
    adj_int = tiles[0]
    adj = adj_int.astype(jnp.bfloat16)
    picked = jnp.take(source, src, axis=0)
    prod = jnp.einsum("tij,tjf->tif", adj, picked, preferred_element_type=jnp.float32)
    neigh = jax.ops.segment_sum(prod, dst, num_segments=own_blocks).reshape(rows_own, width)
    degree = jax.ops.segment_sum(
        jnp.sum(adj_int, axis=2).astype(jnp.float32), dst, num_segments=own_blocks
    ).reshape(rows_own)
    scale = 1.0 / (1.0 + degree)
    agg = (neigh * scale[:, None]).astype(jnp.bfloat16)
    pre = (
        jnp.dot(features, w_self, preferred_element_type=jnp.float32)
        + jnp.dot(agg, w_neigh, preferred_element_type=jnp.float32)
        + bias
    )
    sig = jax.nn.sigmoid(pre)
    layer_out = (pre * sig).astype(jnp.bfloat16)
    dpre = cotangent.astype(jnp.float32) * (sig * (1.0 + pre * (1.0 - sig)))
    dpre_b = dpre.astype(jnp.bfloat16)
    term_self = lax.dot_general(
        features, dpre_b, (((0,), (0,)), ((), ())), preferred_element_type=jnp.float32
    )
    term_neigh = lax.dot_general(
        agg, dpre_b, (((0,), (0,)), ((), ())), preferred_element_type=jnp.float32
    )
    term_bias = jnp.sum(dpre, axis=0)
    g_rows = lax.dot_general(
        dpre_b, w_neigh, (((1,), (1,)), ((), ())), preferred_element_type=jnp.float32
    )
    g_rows = (g_rows * scale[:, None]).astype(jnp.bfloat16)
    g_blocks = jnp.take(g_rows.reshape(own_blocks, tile_rows, width), dst, axis=0)
    back = jnp.einsum("tij,tif->tjf", adj, g_blocks, preferred_element_type=jnp.float32)
    back_sum = jax.ops.segment_sum(back, src, num_segments=src_blocks).reshape(
        src_blocks * tile_rows, width
    )
    back_b = back_sum[rows_own:].astype(jnp.bfloat16)
    returned = move_grads(back_b.reshape(peers, tile_rows, width))
    returned = returned.reshape(peers * tile_rows, width).astype(jnp.float32) * keep[
        :, None
    ].astype(jnp.float32)
    self_grad = lax.dot_general(
        dpre_b, w_self, (((1,), (1,)), ((), ())), preferred_element_type=jnp.float32
    )
    grad_features = (
        self_grad
        + back_sum[:rows_own]
        + jax.ops.segment_sum(returned, flat_picks, num_segments=rows_own)
    )
    total_self, total_neigh, total_bias = lax.psum(
        (term_self, term_neigh, term_bias), ("row", "col")
    )
    inv_root = 1.0 / jnp.sqrt(jnp.float32(rows_own * lax.axis_size(("row", "col"))))
    return (
        layer_out,
        grad_features,
        total_self * inv_root,
        total_neigh * inv_root,
        total_bias * inv_root,
    )


def solution(mesh):
    in_specs = (
        P(("row", "col"), None),
        P(("row", "col"), None, None),
        P(("row", "col"), None),
        P(("row", "col"), None),
        P(("row", "col"), None),
        P(("row", "col"), None, None, None),
        P(),
        P(),
        P(),
        P(("row", "col"), None),
    )
    out_specs = (P(("row", "col"), None), P(("row", "col"), None), P(), P(), P())
    return jax.shard_map(
        on_device, mesh=mesh, in_specs=in_specs, out_specs=out_specs, check_vma=False
    )
```

profile of v0, /device:TPU:0, one launch (start us, length us, event | category | flops | bytes accessed | tf_op | source)
XLA Modules:
  0.0 379.1 jit_solution(15681713276999709895)
XLA Ops:
  8.8 14.9 %gather_fusion = bf16[4096,256]{1,0:T(8,128)(2,1)S(1)} fusion(bf16[4096,256]{1,0:T(8,128)(2,1)} %param.10, s32[4096]{0:T(1024)S(1)} %broadcast_clamp_fusion), kind=kCustom, calls=%fused_computation | custom fusion | bytes 4210688 | tf_op jit(solution)/shard_map/jit(_take)/gather | solution.py:27
  23.6 2.6 select_multiply_fusion
  26.3 7.5 %all-to-all-start = ((bf16[32,128,256]{2,1,0:T(8,128)(2,1)}), bf16[32,128,256]{2,1,0:T(8,128)(2,1)}, u32[]{:S(2)}, u32[]{:S(2)}) async-start(bf16[32,128,256]{2,1,0:T(8,128)(2,1)} %select_multiply_fusion), calls=%async_computation | async-start | bytes 4194304 | tf_op jit(solution)/shard_map/all_to_all | solution.py:8
  33.8 3.3 reduce_sum.18
  37.1 1.0 scatter_custom_fusion.1
  38.2 2.7 fusion.32
  40.9 42.8 %all-to-all-done = bf16[32,128,256]{2,1,0:T(8,128)(2,1)} async-done(((bf16[32,128,256]{2,1,0:T(8,128)(2,1)}), bf16[32,128,256]{2,1,0:T(8,128)(2,1)}, u32[]{:S(2)}, u32[]{:S(2)}) %all-to-all-start) | async-done | bytes 2097184 | tf_op jit(solution)/shard_map/all_to_all | solution.py:8
  83.8 3.8 %pad_maximum_fusion = bf16[8192,256]{1,0:T(8,128)(2,1)} fusion(bf16[4096,256]{1,0:T(8,128)(2,1)} %bitcast.7, bf16[4096,256]{1,0:T(8,128)(2,1)S(1)} %copy-done.2), kind=kLoop, calls=%fused_computation.13 | loop fusion | flops 8388608 | bytes 8388608 | tf_op jit(solution)/shard_map/concatenate | solution.py:29
  87.6 5.0 %gather_fusion.1 = bf16[64,128,256]{2,1,0:T(8,128)(2,1)} fusion(bf16[64,128,256]{2,1,0:T(8,128)(2,1)} %bitcast.59, s32[1024]{0:T(1024)S(1)} %pad_clamp_fusion.1), kind=kCustom, calls=%fused_computation.1 | custom fusion | bytes 8388864 | tf_op jit(solution)/shard_map/jit(_take)/gather | solution.py:35
  92.5 8.2 %fusion.10 = f32[64,128,256]{1,2,0:T(8,128)} fusion(bf16[64,128,256]{2,1,0:T(8,128)(2,1)} %gather_fusion.1, pred[64]{0:T(512)(128)(4,1)S(1)} %compare_and_fusion.2, s32[1,64,128,128]{3,2,1,0:T(8,128)} %param.15), kind=kOutput, calls=%fused_computation.27 | convolution fusion | flops 540016640 | bytes 16777280 | tf_op jit(solution)/shard_map/tij,tjf->tif/dot_general | solution.py:36
  100.7 9.0 %copy.21 = f32[64,128,256]{2,1,0:T(8,128)} copy(f32[64,128,256]{1,2,0:T(8,128)} %fusion.10) | data formatting | bytes 16777216 | tf_op jit(solution)/shard_map/tij,tjf->tif/dot_general | solution.py:36
  109.7 2.5 broadcast_in_dim.40
  112.2 19.3 %scatter_fusion = f32[32,128,256]{2,1,0:T(8,128)} fusion(f32[32,128,256]{2,1,0:T(8,128)} %broadcast_in_dim.40, s32[64]{0:T(128)S(1)} %bitcast.67, f32[64,128,256]{2,1,0:T(8,128)} %copy.21), kind=kCustom, calls=%fused_computation.3 | custom fusion | flops 2097152 | bytes 25166080 | tf_op jit(solution)/shard_map/scatter-add | solution.py:37
  131.5 2.7 fusion.3
  135.6 3.4 fusion.31
  139.0 1.3 copy-done.4
  140.4 2.0 fusion.1
  142.4 4.4 %gather_fusion.2 = bf16[64,128,256]{2,1,0:T(8,128)(2,1)} fusion(bf16[32,128,256]{2,1,0:T(8,128)(2,1)} %bitcast.58, s32[1024]{0:T(1024)S(1)} %pad_clamp_fusion), kind=kCustom, calls=%fused_computation.2 | custom fusion | bytes 8388864 | tf_op jit(solution)/shard_map/jit(_take)/gather | solution.py:63
  146.8 8.2 %fusion.13 = f32[64,128,256]{1,2,0:T(8,128)} fusion(bf16[64,128,256]{2,1,0:T(8,128)(2,1)} %gather_fusion.2, pred[64]{0:T(512)(128)(4,1)S(1)} %compare_and_fusion.1, s32[1,64,128,128]{3,2,1,0:T(8,128)} %param.15), kind=kOutput, calls=%fused_computation.28 | convolution fusion | flops 540016640 | bytes 16777280 | tf_op jit(solution)/shard_map/tij,tif->tjf/dot_general | solution.py:64
  155.0 9.0 %copy.23 = f32[64,128,256]{2,1,0:T(8,128)} copy(f32[64,128,256]{1,2,0:T(8,128)} %fusion.13) | data formatting | bytes 16777216 | tf_op jit(solution)/shard_map/tij,tif->tjf/dot_general | solution.py:64
  164.0 4.2 %broadcast_in_dim.45 = f32[64,128,256]{2,1,0:T(8,128)} broadcast(f32[]{:T(128)} %constant.24.clone.1), dimensions={} | broadcast | bytes 8388612 | tf_op jit(solution)/shard_map/broadcast_in_dim | solution.py:65
  168.2 19.7 %scatter_fusion.1 = f32[64,128,256]{2,1,0:T(8,128)} fusion(f32[64,128,256]{2,1,0:T(8,128)} %broadcast_in_dim.45, s32[64]{0:T(128)S(1)} %bitcast.68, f32[64,128,256]{2,1,0:T(8,128)} %copy.23), kind=kCustom, calls=%fused_computation.5 | custom fusion | flops 2097152 | bytes 25166080 | tf_op jit(solution)/shard_map/scatter-add | solution.py:65
  187.9 3.8 slice.23
  191.7 3.5 all-to-all-start.1
  195.5 4.8 %slice.20 = f32[32,128,256]{2,1,0:T(8,128)} slice(f32[64,128,256]{2,1,0:T(8,128)} %scatter_fusion.1), slice={[0:32], [0:128], [0:256]} | slice | bytes 8388608 | tf_op jit(solution)/shard_map/slice | solution.py:78
  200.3 1.6 fusion.33
  201.9 1.4 convolution_bitcast_fusion
  203.4 5.6 %convolution_add_fusion = f32[4096,256]{1,0:T(8,128)} fusion(f32[4096,256]{1,0:T(8,128)} %bitcast.60, bf16[4096,256]{1,0:T(8,128)(2,1)} %copy-done.4, bf16[256,256]{1,0:T(8,128)(2,1)S(1)} %copy-done.8), kind=kOutput, calls=%fused_computation.8 | convolution fusion | flops 537919488 | bytes 10616832 | tf_op jit(solution)/shard_map/dot_general | solution.py:73
  209.0 57.6 %psum.23 = f32[256]{0:T(256)S(1)} all-reduce(f32[256]{0:T(256)S(1)} %get-tuple-element.17), channel_id=1, replica_groups=mesh['row'=4,'col'=8] {'row','col'}, use_global_device_ids=true, to_apply=%region_8.9 | all-reduce | flops 256 | bytes 2048 | tf_op jit(solution)/shard_map/psum | solution.py:81
  267.1 72.5 %all-reduce.3.cloned.1.call-done = (f32[256,256]{0,1:T(8,128)}, f32[256,256]{0,1:T(8,128)}) async-done(((f32[256,256]{0,1:T(8,128)}, f32[256,256]{0,1:T(8,128)}), (f32[256,256]{0,1:T(8,128)}, f32[256,256]{0,1:T(8,128)})) %all-reduce.3.cloned.1.call-update) | async-done | bytes 524304 | tf_op jit(solution)/shard_map/psum | solution.py:81
  339.6 1.0 broadcast_multiply_fusion.1
  343.3 29.0 %scatter_custom_fusion.3 = f32[4096,256]{1,0:T(8,128)} fusion(f32[4096,256]{1,0:T(8,128)} %convolution_add_fusion, s32[4096]{0:T(1024)} %bitcast.64, bf16[4096,256]{1,0:T(8,128)(2,1)} %bitcast.24, f32[4096]{0:T(1024)S(1)} %get-tuple-element.20), kind=kCustom, calls=%fused_computation.15 | custom fusion | flops 3145728 | bytes 6307840 | tf_op jit(solution)/shard_map/scatter-add | solution.py:79
  (42 shorter events, 6.5 us)
Async XLA Ops:
  7.2 127.1 %copy-start = (bf16[256,256]{1,0:T(8,128)(2,1)S(1)}, bf16[256,256]{1,0:T(8,128)(2,1)}, u32[]{:S(2)}) copy-start(bf16[256,256]{1,0:T(8,128)(2,1)} %param.17) | copy-start | bytes 393220
  26.3 10.8 %copy-start.9 = (s32[1,64]{1,0:T(1,128)S(1)}, s32[1,64]{1,0:T(1,128)}, u32[]{:S(2)}) copy-start(s32[1,64]{1,0:T(1,128)} %param.13) | copy-start | bytes 772
  26.3 11.8 %copy-start.10 = (s32[1,64]{1,0:T(1,128)S(1)}, s32[1,64]{1,0:T(1,128)}, u32[]{:S(2)}) copy-start(s32[1,64]{1,0:T(1,128)} %param.14) | copy-start | bytes 772
  26.3 11.9 %copy-start.2 = (bf16[4096,256]{1,0:T(8,128)(2,1)S(1)}, bf16[4096,256]{1,0:T(8,128)(2,1)}, u32[]{:S(2)}) copy-start(bf16[4096,256]{1,0:T(8,128)(2,1)} %param.10) | copy-start | bytes 6291460
  26.3 11.9 %copy-start.8 = (bf16[256,256]{1,0:T(8,128)(2,1)S(1)}, bf16[256,256]{1,0:T(8,128)(2,1)}, u32[]{:S(2)}) copy-start(bf16[256,256]{1,0:T(8,128)(2,1)} %param.16) | copy-start | bytes 393220
  26.3 57.5 %all-to-all-start = ((bf16[32,128,256]{2,1,0:T(8,128)(2,1)}), bf16[32,128,256]{2,1,0:T(8,128)(2,1)}, u32[]{:S(2)}, u32[]{:S(2)}) async-start(bf16[32,128,256]{2,1,0:T(8,128)(2,1)} %select_multiply_fusion), calls=%async_computation | async-start | bytes 4194304 | tf_op jit(solution)/shard_map/all_to_all | solution.py:8
  131.5 3.4 copy-start.3
  131.5 4.1 %copy-start.11 = (bf16[4096,256]{1,0:T(8,128)(2,1)S(1)}, bf16[4096,256]{1,0:T(8,128)(2,1)}, u32[]{:S(2)}) copy-start(bf16[4096,256]{1,0:T(8,128)(2,1)} %param.19) | copy-start | bytes 6291460
  131.5 4.1 %copy-start.12 = (f32[256]{0:T(256)S(1)}, f32[256]{0:T(256)}, u32[]{:S(2)}) copy-start(f32[256]{0:T(256)} %param.18) | copy-start | bytes 3076
  135.6 3.4 copy-start.6
  139.0 1.3 copy-start.4
  191.7 151.6 %all-to-all-start.1 = ((bf16[32,128,256]{2,1,0:T(8,128)(2,1)}), bf16[32,128,256]{2,1,0:T(8,128)(2,1)}, u32[]{:S(2)}, u32[]{:S(2)}) async-start(bf16[32,128,256]{2,1,0:T(8,128)(2,1)} %slice.23), calls=%async_computation.1 | async-start | bytes 4194304 | tf_op jit(solution)/shard_map/all_to_all | solution.py:12
  195.2 144.4 %all-reduce.3.cloned.1.call-start = ((), (), s32[]{:S(2)}) async-start(), calls=%async_computation.2 | async-start | bytes 1048576 | tf_op jit(solution)/shard_map/psum | solution.py:81
  195.4 4.8 %copy-start.5 = (bf16[4096,256]{1,0:T(8,128)(2,1)S(1)}, bf16[4096,256]{1,0:T(8,128)(2,1)}, u32[]{:S(2)}) copy-start(bf16[4096,256]{1,0:T(8,128)(2,1)} %copy-done.4) | copy-start | bytes 6291460
  195.5 4.8 %copy-start.7 = (bf16[4096,256]{1,0:T(8,128)(2,1)S(1)}, bf16[4096,256]{1,0:T(8,128)(2,1)}, u32[]{:S(2)}) copy-start(bf16[4096,256]{1,0:T(8,128)(2,1)} %copy-done.6) | copy-start | bytes 6291460
  339.6 32.7 %copy-start.1 = (bf16[256,256]{1,0:T(8,128)(2,1)S(1)}, bf16[256,256]{1,0:T(8,128)(2,1)}, u32[]{:S(2)}) copy-start(bf16[256,256]{1,0:T(8,128)(2,1)} %param.17) | copy-start | bytes 393220
Sparse Core Ops, SparseCore 0:
  203.5 136.0 all-reduce.2
where the time goes:
time: 380 us; the launch traced here: 379 us
  waiting for transfers between devices  115 us (30%)
  other arithmetic  85.7 us (23%)
  local copies, waits for them, and re-layouts  62 us (16%)
  blocking collectives  57.6 us (15%)
  matrix products  33.2 us (9%)
  between operations  14.2 us (4%)
  starting transfers between devices  11.2 us (3%)
    psum x1, waiting for transfers between devices, on_device(): lax.psum((term_self, term_neigh, term_bias), ('row', 'col'))  72.5 us
    psum x1, blocking collectives, on_device(): lax.psum((term_self, term_neigh, term_bias), ('row', 'col'))  57.6 us
    all_to_all x1, waiting for transfers between devices, move_rows(): lax.all_to_all(block, ('row', 'col'), split_axis=0, concat_axis=0, tiled=...  42.8 us
    scatter-add x1, other arithmetic, on_device(): jax.ops.segment_sum(returned, flat_picks, num_segments=rows_own)  29 us
    scatter-add x1, other arithmetic, on_device(): jax.ops.segment_sum(back, src, num_segments=src_blocks)  19.7 us
    scatter-add x1, other arithmetic, on_device(): jax.ops.segment_sum(prod, dst, num_segments=own_blocks)  19.3 us
    gather x1, local copies, waits for them, and re-layouts, on_device(): jnp.take(features, flat_picks, axis=0) * keep[:, None].astype(jnp.bfloat16)  14.9 us
    dot_general x1, local copies, waits for them, and re-layouts, on_device(): jnp.einsum('tij,tjf->tif', adj, picked, preferred_element_type=jnp.float32)  9 us
  transfers between devices with their start and end apart: 3, of which 2 were waited for; matrix products, arithmetic and copies ran while one was open for 7% of the time, Pallas kernels for 0%

commit v1 on v0

v1 whole, which is shorter than its diff:
```python
import functools

import jax
import jax.numpy as jnp
from jax import lax
from jax.experimental import pallas as pl
from jax.experimental.pallas import tpu as pltpu
from jax.sharding import PartitionSpec as P

AXES = ("row", "col")
LANES = 128
VMEM = pl.BlockSpec(memory_space=pltpu.VMEM)
SMEM = pl.BlockSpec(memory_space=pltpu.SMEM)
ANY = pl.BlockSpec(memory_space=pl.ANY)
F32 = jnp.float32
BF16 = jnp.bfloat16


def matmul(a, b):
    return jnp.dot(a, b, preferred_element_type=F32)


def matmul_t(a, b):
    return lax.dot_general(a, b, (((1,), (1,)), ((), ())), preferred_element_type=F32)


def params(mib):
    return pltpu.CompilerParams(vmem_limit_bytes=mib * 1024 * 1024)


def cost(flops, nbytes):
    return pl.CostEstimate(flops=int(flops), bytes_accessed=int(nbytes), transcendentals=0)


def gather_kernel(picks_in, counts_in, x_in, out_in, picks, counts, x, out, sems, *scratch):
    rows, width = x.shape
    peers, slots = picks.shape
    halves = width // LANES
    wide, stage = scratch[:halves], scratch[halves:]
    parts = 4
    chunk = rows // parts
    step = 128
    copies = [
        pltpu.make_async_copy(picks_in, picks, sems.at[0]),
        pltpu.make_async_copy(counts_in, counts, sems.at[1]),
    ]
    for c in range(parts):
        at = pl.ds(c * chunk, chunk)
        copies.append(pltpu.make_async_copy(x_in.at[at], x.at[at], sems.at[2 + c]))
    for copy in copies:
        copy.start()
    for c in range(parts):
        copies[2 + c].wait()

        @pl.loop(c * chunk // step, (c + 1) * chunk // step)
        def _(i):
            at = pl.ds(pl.multiple_of(i * step, step), step)
            for h in range(halves):
                wide[h][at, :] = x[at, h * LANES : (h + 1) * LANES].astype(F32)

    copies[0].wait()
    copies[1].wait()

    @pl.loop(0, peers)
    def _(p):
        for k in range(slots):
            row = picks[p, k]
            for h in range(halves):
                stage[h][pl.ds(k, 1), :] = wide[h][pl.ds(row, 1), :]
        used = lax.broadcasted_iota(jnp.int32, (slots, LANES), 0) < counts[0, p]
        for h in range(halves):
            value = jnp.where(used, stage[h][...], 0.0)
            out[p, :, h * LANES : (h + 1) * LANES] = value.astype(BF16)
        pltpu.make_async_copy(out.at[p], out_in.at[p], sems.at[2 + parts]).start()

    pltpu.make_async_copy(out, out_in, sems.at[2 + parts]).wait()


def gather_rows(x, picks, counts):
    rows, width = x.shape
    peers, slots = picks.shape
    halves = width // LANES
    return pl.pallas_call(
        gather_kernel,
        out_shape=jax.ShapeDtypeStruct((peers, slots, width), BF16),
        in_specs=[ANY, ANY, ANY],
        out_specs=ANY,
        scratch_shapes=[
            pltpu.SMEM(picks.shape, jnp.int32),
            pltpu.SMEM(counts.shape, jnp.int32),
            pltpu.VMEM((rows, width), BF16),
            pltpu.VMEM((peers, slots, width), BF16),
            pltpu.SemaphoreType.DMA((7,)),
        ]
        + [pltpu.VMEM((rows, LANES), F32)] * halves
        + [pltpu.VMEM((slots, LANES), F32)] * halves,
        compiler_params=params(60),
        cost_estimate=cost(1e10, 4 * rows * width),
        name="gather_rows",
    )(picks, counts, x)


def local_kernel(src, dst, tiles, x, edge, edge_t, own_t, by_src, neigh, scale, order):
    count, tb, _ = tiles.shape
    own = neigh.shape[0]

    @pl.loop(0, count)
    def _(t):
        order[src[0, t]] = t

    neigh[...] = jnp.zeros_like(neigh)
    scale[...] = jnp.zeros_like(scale)
    ones = jnp.ones((8, tb), BF16)

    @pl.loop(0, own)
    def _(s):
        t = order[s]
        d = dst[0, t]
        by_src[s] = d
        tile = tiles[t].astype(F32)
        adj = tile.astype(BF16)
        own_t[s] = tile.T.astype(BF16)
        at = pl.ds(pl.multiple_of(s * tb, tb), tb)
        neigh[d] += matmul(adj, x[at, :])
        scale[d] += matmul_t(ones, adj)

    @pl.loop(own, count)
    def _(s):
        t = order[s]
        d = dst[0, t]
        by_src[s] = d
        tile = tiles[t].astype(F32)
        adj = tile.astype(BF16)
        edge[s - own] = adj
        edge_t[s - own] = tile.T.astype(BF16)
        scale[d] += matmul_t(ones, adj)

    scale[...] = 1.0 / (1.0 + scale[...])


def local_work(src, dst, tiles, x):
    count, tb, _ = tiles.shape
    rows, width = x.shape
    own = rows // tb
    edges = count - own
    return pl.pallas_call(
        local_kernel,
        out_shape=(
            jax.ShapeDtypeStruct((edges, tb, tb), BF16),
            jax.ShapeDtypeStruct((edges, tb, tb), BF16),
            jax.ShapeDtypeStruct((own, tb, tb), BF16),
            jax.ShapeDtypeStruct((count,), jnp.int32),
            jax.ShapeDtypeStruct((own, tb, width), F32),
            jax.ShapeDtypeStruct((own, 8, tb), F32),
        ),
        in_specs=[SMEM, SMEM, VMEM, VMEM],
        out_specs=(VMEM, VMEM, VMEM, SMEM, VMEM, VMEM),
        scratch_shapes=[pltpu.SMEM((count,), jnp.int32)],
        compiler_params=params(48),
        cost_estimate=cost(2e10, 4 * tiles.size),
        name="local_work",
    )(src, dst, tiles, x)


def spread_scale(scale, scale_v):
    own, _, tb = scale.shape

    @pl.loop(0, own, unroll=4)
    def _(s):
        scale_v[s] = jnp.broadcast_to(scale[s, 0:1, :], (tb, tb)).T


def rates_of(scale_v, which, size, width):
    rate = scale_v[which].reshape(size, scale_v.shape[2])
    return jnp.concatenate([rate] * (width // scale_v.shape[2]), 1)


def activation(x, agg, cot, w_self, w_neigh, bias):
    pre = matmul(x, w_self) + matmul(agg, w_neigh) + bias
    sig = 0.5 * jnp.tanh(0.5 * pre) + 0.5
    dpre = cot.astype(F32) * (sig * (1.0 + pre * (1.0 - sig)))
    return pre * sig, dpre


def middle_kernel(
    by_src, arrived, edge, edge_t, neigh, x, cot, scale, w_self, w_neigh, bias,
    agg_out, back_out,
    arrived_v, edge_v, edge_tv, product, acc, scale_v, x_v, cot_v, agg_v, g_v, back_v, sems,
):
    own, tb, width = acc.shape
    edges = product.shape[0]
    rows = own * tb
    parts = 4
    number = iter(range(sems.shape[0]))

    def start(source, target):
        copy = pltpu.make_async_copy(source, target, sems.at[next(number)])
        copy.start()
        return copy

    def cuts(size):
        return [pl.ds(c * (size // parts), size // parts) for c in range(parts)]

    def start_cuts(source, target, size):
        return [start(source.at[at], target.at[at]) for at in cuts(size)]

    coming = []
    for at in cuts(edges):
        coming.append(
            (start(edge.at[at], edge_v.at[at]), start(arrived.at[at], arrived_v.at[at]))
        )
    in_neigh = start(neigh, acc)
    nodes = start_cuts(x, x_v, rows)
    cots = start_cuts(cot, cot_v, rows)
    in_edge_t = start(edge_t, edge_tv)
    spread_scale(scale, scale_v)

    each = edges // parts
    for c in range(parts):
        for copy in coming[c]:
            copy.wait()

        @pl.loop(c * each, (c + 1) * each, unroll=4)
        def _(s):
            product[s] = matmul(edge_v[s], arrived_v[s])

    in_neigh.wait()

    @pl.loop(0, edges)
    def _(s):
        acc[by_src[own + s]] += product[s]

    block = 4
    size = block * tb
    leaving = []
    for c in range(parts):
        nodes[c].wait()
        cots[c].wait()

        @pl.loop(c * (own // parts) // block, (c + 1) * (own // parts) // block)
        def _(i):
            at = pl.ds(pl.multiple_of(i * size, size), size)
            which = pl.ds(i * block, block)
            rate = rates_of(scale_v, which, size, width)
            agg = (acc[which].reshape(size, width) * rate).astype(BF16)
            agg_v[at, :] = agg
            _, dpre = activation(
                x_v[at, :], agg, cot_v[at, :], w_self[...], w_neigh[...], bias[...]
            )
            g = (matmul_t(dpre.astype(BF16), w_neigh[...]) * rate).astype(BF16)
            g_v[which] = g.reshape(block, tb, width)

        at = cuts(rows)[c]
        leaving.append(start(agg_v.at[at], agg_out.at[at]))

    in_edge_t.wait()
    for c in range(parts):

        @pl.loop(c * each, (c + 1) * each, unroll=4)
        def _(s):
            back_v[s] = matmul(edge_tv[s], g_v[by_src[own + s]]).astype(BF16)

        at = cuts(edges)[c]
        leaving.append(start(back_v.at[at], back_out.at[at]))
    for copy in leaving:
        copy.wait()


def middle_work(by_src, arrived, edge, edge_t, neigh, x, cot, scale, w_self, w_neigh, bias):
    own, tb, width = neigh.shape
    edges = edge.shape[0]
    rows, hidden = cot.shape
    return pl.pallas_call(
        middle_kernel,
        out_shape=(
            jax.ShapeDtypeStruct((rows, width), BF16),
            jax.ShapeDtypeStruct((edges, tb, width), BF16),
        ),
        in_specs=[SMEM] + [ANY] * 6 + [VMEM] * 4,
        out_specs=(ANY, ANY),
        scratch_shapes=[
            pltpu.VMEM((edges, tb, width), BF16),
            pltpu.VMEM((edges, tb, tb), BF16),
            pltpu.VMEM((edges, tb, tb), BF16),
            pltpu.VMEM((edges, tb, width), F32),
            pltpu.VMEM((own, tb, width), F32),
            pltpu.VMEM((own, tb, tb), F32),
            pltpu.VMEM((rows, width), BF16),
            pltpu.VMEM((rows, hidden), BF16),
            pltpu.VMEM((rows, width), BF16),
            pltpu.VMEM((own, tb, width), BF16),
            pltpu.VMEM((edges, tb, width), BF16),
            pltpu.SemaphoreType.DMA((32,)),
        ],
        compiler_params=params(60),
        cost_estimate=cost(2e10, 16 * rows * width),
        name="middle_work",
    )(by_src, arrived, edge, edge_t, neigh, x, cot, scale, w_self, w_neigh, bias)


def tail_kernel(
    agg, x, cot, scale, w_self, w_neigh, bias, layer_out, dpre_out, g_out, terms, scale_v
):
    rows, width = x.shape
    own, tb, _ = g_out.shape
    hidden = cot.shape[1]
    spread_scale(scale, scale_v)
    terms[...] = jnp.zeros_like(terms)
    block = 4
    size = block * tb

    @pl.loop(0, own // block)
    def _(i):
        at = pl.ds(pl.multiple_of(i * size, size), size)
        which = pl.ds(i * block, block)
        near = agg[at, :]
        layer, dpre = activation(
            x[at, :], near, cot[at, :], w_self[...], w_neigh[...], bias[...]
        )
        layer_out[at, :] = layer.astype(BF16)
        dpre_b = dpre.astype(BF16)
        dpre_out[at, :] = dpre_b
        rate = rates_of(scale_v, which, size, width)
        g = (matmul_t(dpre_b, w_neigh[...]) * rate).astype(BF16)
        g_out[which] = g.reshape(block, tb, width)
        dims = (((0,), (0,)), ((), ()))
        terms[:width, :] += lax.dot_general(x[at, :], dpre_b, dims, preferred_element_type=F32)
        terms[width : 2 * width, :] += lax.dot_general(
            near, dpre_b, dims, preferred_element_type=F32
        )
        terms[2 * width : 2 * width + 8, :] += jnp.sum(dpre.reshape(size // 8, 8, hidden), axis=0)


def tail_work(agg, x, cot, scale, w_self, w_neigh, bias, spare):
    rows, width = x.shape
    own, _, tb = scale.shape
    hidden = cot.shape[1]
    return pl.pallas_call(
        tail_kernel,
        out_shape=(
            jax.ShapeDtypeStruct((rows, hidden), BF16),
            jax.ShapeDtypeStruct((rows, hidden), BF16),
            jax.ShapeDtypeStruct((own, tb, width), BF16),
            jax.ShapeDtypeStruct((2 * width + spare, hidden), F32),
        ),
        in_specs=[VMEM] * 7,
        out_specs=(VMEM,) * 4,
        scratch_shapes=[pltpu.VMEM((own, tb, tb), F32)],
        compiler_params=params(40),
        cost_estimate=cost(1e10, 16 * rows * width),
        name="tail_work",
    )(agg, x, cot, scale, w_self, w_neigh, bias)


def own_kernel(by_src, own_t, g, dpre_b, w_self, out):
    own, tb, width = g.shape

    @pl.loop(0, own, unroll=4)
    def _(s):
        at = pl.ds(pl.multiple_of(s * tb, tb), tb)
        back = matmul(own_t[s], g[by_src[s]])
        out[at, :] = back + matmul_t(dpre_b[at, :], w_self[...])


def own_work(by_src, own_t, g, dpre_b, w_self):
    own, tb, width = g.shape
    return pl.pallas_call(
        own_kernel,
        out_shape=jax.ShapeDtypeStruct((own * tb, width), F32),
        in_specs=[SMEM] + [VMEM] * 4,
        out_specs=VMEM,
        compiler_params=params(24),
        cost_estimate=cost(1e10, 10 * own * tb * width),
        name="own_work",
    )(by_src, own_t, g, dpre_b, w_self)


def scatter_kernel(picks, base, returned_in, out_in, returned, out, sems):
    rows, width = base.shape
    count = picks.shape[1]
    parts = 4
    depth = count // parts
    block = 512
    coming = []
    for c in range(parts):
        at = pl.ds(c * depth, depth)
        coming.append(pltpu.make_async_copy(returned_in.at[at], returned.at[at], sems.at[c]))
    for copy in coming:
        copy.start()
    for copy in coming:
        copy.wait()
    inner = 512

    def send(i):
        at = pl.ds(pl.multiple_of(i * block, block), block)
        return pltpu.make_async_copy(out.at[at], out_in.at[at], sems.at[parts])

    @pl.loop(0, rows // block)
    def _(i):
        at = pl.ds(pl.multiple_of(i * block, block), block)
        here = lax.broadcasted_iota(jnp.int32, (block, inner), 0) + i * block
        total = base[at, :]
        for k in range(count // inner):
            hit = here == picks[:, k * inner : (k + 1) * inner]
            hot = jnp.where(hit, 1.0, 0.0).astype(BF16)
            total += matmul(hot, returned[k * inner : (k + 1) * inner, :])
        out[at, :] = total
        send(i).start()

    pltpu.make_async_copy(out, out_in, sems.at[parts]).wait()


def scatter_rows(picks, base, returned):
    rows, width = base.shape
    return pl.pallas_call(
        scatter_kernel,
        out_shape=jax.ShapeDtypeStruct((rows, width), F32),
        in_specs=[VMEM, VMEM, ANY],
        out_specs=ANY,
        scratch_shapes=[
            pltpu.VMEM(returned.shape, BF16),
            pltpu.VMEM((rows, width), F32),
            pltpu.SemaphoreType.DMA((5,)),
        ],
        compiler_params=params(32),
        cost_estimate=cost(1e10, 10 * rows * width),
        name="scatter_rows",
    )(picks, base, returned)


def exchange(block, groups=None):
    return lax.all_to_all(block, AXES, 0, 0, tiled=True, axis_index_groups=groups)


def flip(value, bit, members):
    return lax.ppermute(value, AXES, [(i, i ^ bit) for i in range(members)])


def split_bits(shape):
    n_row, n_col = shape
    inner = n_col // 4 if n_col % 4 == 0 else n_col
    near = [1 << i for i in range(inner.bit_length() - 1)]
    near += [n_col << i for i in range(n_row.bit_length() - 1)]
    return near, [inner * i for i in range(1, n_col // inner)]


def share_of_total(terms, shape):
    members = shape[0] * shape[1]
    near, far = split_bits(shape)
    me = lax.axis_index(AXES)
    for bit in near:
        upper = (me & bit) != 0
        half = terms.shape[0] // 2
        low, high = terms[:half], terms[half:]
        terms = jnp.where(upper, high, low) + flip(jnp.where(upper, low, high), bit, members)
    levels = [terms] + [flip(terms, bits, members) for bits in far]
    while len(levels) > 1:
        levels = [levels[i] + levels[i + 1] for i in range(0, len(levels), 2)]
    return levels[0]


def join_shares(share, shape):
    members = shape[0] * shape[1]
    near, _ = split_bits(shape)

    def place(device):
        return sum(1 << (len(near) - 1 - i) for i, bit in enumerate(near) if device & bit)

    mask = sum(near)
    planes = {}
    for device in range(members):
        planes.setdefault(device & ~mask, []).append(device)
    groups = [sorted(plane, key=place) for _, plane in sorted(planes.items())]
    count = len(groups[0])
    whole = exchange(jnp.broadcast_to(share[None], (count,) + share.shape), groups)
    return whole.reshape(count * share.shape[0], share.shape[1])


def on_device(
    shape, features, send_rows, counts, tile_dst, tile_src, tiles, w_self, w_neigh, bias, cotangent
):
    rows, width = features.shape
    peers, slots = send_rows.shape[1:]
    picks = send_rows[0]
    outgoing = gather_rows(features, picks, counts)
    arrived = exchange(outgoing)
    edge, edge_t, own_t, by_src, neigh, scale = local_work(tile_src, tile_dst, tiles[0], features)
    keep = jnp.arange(slots, dtype=jnp.int32)[None, :] < counts[0][:, None]
    targets = jnp.where(keep, picks, -1).reshape(1, peers * slots)
    agg, back_b = middle_work(
        by_src, arrived, edge, edge_t, neigh, features, cotangent, scale, w_self, w_neigh, bias[None]
    )
    returned = exchange(back_b).reshape(peers * slots, width)
    spare = 8 << len(split_bits(shape)[0])
    layer_out, dpre_b, g, terms = tail_work(
        agg, features, cotangent, scale, w_self, w_neigh, bias[None], spare
    )
    own_grad = own_work(by_src, own_t, g, dpre_b, w_self)
    share = share_of_total(terms, shape)
    share, returned = lax.optimization_barrier((share, returned))
    terms = join_shares(share, shape)
    bias_total = jnp.sum(terms[2 * width : 2 * width + 8], axis=0)
    grad_features = scatter_rows(targets, own_grad, returned)
    inv_root = 1.0 / jnp.sqrt(F32(rows * shape[0] * shape[1]))
    return (
        layer_out,
        grad_features,
        terms[:width] * inv_root,
        terms[width : 2 * width] * inv_root,
        bias_total * inv_root,
    )


def solution(mesh):
    both = P(AXES)
    in_specs = (both,) * 6 + (P(),) * 3 + (both,)
    out_specs = (both, both, P(), P(), P())
    shape = (mesh.shape["row"], mesh.shape["col"])
    return jax.shard_map(
        functools.partial(on_device, shape),
        mesh=mesh,
        in_specs=in_specs,
        out_specs=out_specs,
        check_vma=False,
    )
```

time: 380 us -> 154 us (0.41)
  other arithmetic: 85.7 us -> 1.71 us
  waiting for transfers between devices: 115 us -> 52.2 us
  blocking collectives: 57.6 us -> 0 us
  Pallas kernels: 0 us -> 57.3 us
  local copies, waits for them, and re-layouts: 62 us -> 19.5 us
  matrix products: 33.2 us -> 0 us
  between operations: 14.2 us -> 0.9 us
  starting transfers between devices: 11.2 us -> 22.1 us
    psum x1 -> x0, waiting for transfers between devices: 72.5 us -> none  [on_device(): lax.psum((term_self, term_neigh, term_bias), ('row', 'col'))]
    scatter-add x4 -> x0, other arithmetic: 69 us -> none  [the longest x1 29 us: on_device(): jax.ops.segment_sum(returned, flat_picks, num_segments=rows_own)]
    psum x1 -> x0, blocking collectives: 57.6 us -> none  [on_device(): lax.psum((term_self, term_neigh, term_bias), ('row', 'col'))]
    pallas_call x0 -> x6, Pallas kernels: none -> 57.3 us  [the longest x1 15.1 us: local_work(): pl.pallas_call(local_kernel, out_shape=(jax.ShapeDtypeStruct((edges, tb,...]
    dot_general x8 -> x0, matrix products: 33.2 us -> none  [the longest x1 8.19 us: on_device(): jnp.einsum('tij,tjf->tif', adj, picked, preferred_element_type=jnp.float32)]
    gather x3 -> x0, local copies, waits for them, and re-layouts: 24.2 us -> none  [the longest x1 14.9 us: on_device(): jnp.take(features, flat_picks, axis=0) * keep[:, None].astype(jnp.bfloat16)]
    ppermute x0 -> x6, waiting for transfers between devices: none -> 21.6 us  [flip(): return lax.ppermute(value, AXES, [(i, i ^ bit) for i in range(members)])]
    dot_general x2 -> x0, local copies, waits for them, and re-layouts: 18 us -> none  [the longest x1 9 us: on_device(): jnp.einsum('tij,tjf->tif', adj, picked, preferred_element_type=jnp.float32)]
  transfers between devices with their start and end apart: 3 -> 9, of which waited for: 2 -> 5; matrix products, arithmetic and copies ran while one was open for 7% -> 0% of each run, Pallas kernels for 0% -> 25%
where the time goes in v1:
time: 154 us
  Pallas kernels  57.3 us (37%)
  waiting for transfers between devices  52.2 us (34%)
  starting transfers between devices  22.1 us (14%)
  local copies, waits for them, and re-layouts  19.5 us (13%)
  other arithmetic  1.71 us (1%)
    all_to_all x3, waiting for transfers between devices, exchange(): lax.all_to_all(block, AXES, 0, 0, tiled=True, axis_index_groups=groups)  30.7 us
    ppermute x6, waiting for transfers between devices, flip(): return lax.ppermute(value, AXES, [(i, i ^ bit) for i in range(members)])  21.6 us
    unnamed x50, local copies, waits for them, and re-layouts  18.6 us
    pallas_call x1, Pallas kernels, local_work(): pl.pallas_call(local_kernel, out_shape=(jax.ShapeDtypeStruct((edges, tb,...  15.1 us
    all_to_all x3, starting transfers between devices, exchange(): lax.all_to_all(block, AXES, 0, 0, tiled=True, axis_index_groups=groups)  14.1 us
    pallas_call x1, Pallas kernels, middle_work(): pl.pallas_call(middle_kernel, out_shape=(jax.ShapeDtypeStruct((rows, widt...  12.1 us
    pallas_call x1, Pallas kernels, scatter_rows(): pl.pallas_call(scatter_kernel, out_shape=jax.ShapeDtypeStruct((rows, widt...  11 us
    pallas_call x1, Pallas kernels, tail_work(): pl.pallas_call(tail_kernel, out_shape=(jax.ShapeDtypeStruct((rows, hidden...  8.14 us
  transfers between devices with their start and end apart: 9, of which 5 were waited for; matrix products, arithmetic and copies ran while one was open for 0% of the time, Pallas kernels for 25%

profile of v1, /device:TPU:0, one launch (start us, length us, event | category | flops | bytes accessed | tf_op | source)
XLA Modules:
  0.0 153.7 jit_solution(17350012591464389340)
XLA Ops:
  0.6 7.2 %gather_rows.1 = bf16[32,128,256]{2,1,0:T(8,128)(2,1)} custom-call(s32[32,128]{1,0:T(8,128)} %bitcast.17, s32[1,32]{1,0:T(1,128)} %counts_in.1, bf16[4096,256]{1,0:T(8,128)(2,1)} %x.5), custom_call_target="tpu_custom_call" | custom-call | flops 10000000000 | bytes 4194304 | tf_op jit(solution)/shard_map/gather_rows/pallas_call | solution.py:83
  7.9 7.5 %all-to-all-start = ((bf16[32,128,256]{2,1,0:T(8,128)(2,1)}), bf16[32,128,256]{2,1,0:T(8,128)(2,1)}, u32[]{:S(2)}, u32[]{:S(2)}) async-start(bf16[32,128,256]{2,1,0:T(8,128)(2,1)} %gather_rows.1), calls=%async_computation | async-start | bytes 4194304 | tf_op jit(solution)/shard_map/all_to_all | solution.py:432
  15.4 15.1 %local_work.1 = (bf16[32,128,128]{2,1,0:T(8,128)(2,1)S(1)}, bf16[32,128,128]{2,1,0:T(8,128)(2,1)S(1)}, bf16[32,128,128]{2,1,0:T(8,128)(2,1)S(1)}, s32[64]{0:T(12...) custom-call(s32[1,64]{1,0:T(1,128)S(1)} %copy-done.6, s32[1,64]{1,0:T(1,128)S(1)} %copy-done.7, ...), custom_call_target="tpu_custom_call" | custom-call | flops 20000000000 | bytes 4194304 | tf_op jit(solution)/shard_map/local_work/pallas_call | solution.py:146
  30.6 1.0 copy-done.15
  31.6 1.0 copy-done.17
  32.6 1.0 copy-done.18
  34.7 30.7 %all-to-all-done.arrived = bf16[32,128,256]{2,1,0:T(8,128)(2,1)} async-done(((bf16[32,128,256]{2,1,0:T(8,128)(2,1)}), bf16[32,128,256]{2,1,0:T(8,128)(2,1)}, u32[]{:S(2)}, u32[]{:S(2)}) %all-to-all-start) | async-done | bytes 2097184 | tf_op jit(solution)/shard_map/all_to_all | solution.py:432
  65.4 12.1 %middle_work.1 = (bf16[4096,256]{1,0:T(8,128)(2,1)}, bf16[32,128,256]{2,1,0:T(8,128)(2,1)}) custom-call(s32[64]{0:T(128)} %copy-done.21, bf16[32,128,256]{2,1,0:T(8,128)(2,1)} %all-to-all-done.arrived, bf16[32,128,128]{2,1,0:T(8,128)(2,1)} %copy-done.17, bf16[32,128,128]{2,1,0:T(8,128)(2,1)} %copy-done.18, f32[32,128,256]{2,1,0:T(8,128)} %get-tuple-element.22.neigh, ...), custom_call_target="tpu_custom_call" | custom-call | flops 20000000000 | bytes 16777216 | tf_op jit(solution)/shard_map/middle_work/pallas_call | solution.py:273
  77.6 2.9 %all-to-all-start.1 = ((bf16[32,128,256]{2,1,0:T(8,128)(2,1)}), bf16[32,128,256]{2,1,0:T(8,128)(2,1)S(1)}, u32[]{:S(2)}, u32[]{:S(2)}) async-start(bf16[32,128,256]{2,1,0:T(8,128)(2,1)} %get-tuple-element.30), calls=%async_computation.1 | async-start | bytes 4194304 | tf_op jit(solution)/shard_map/all_to_all | solution.py:432
  80.5 1.6 %copy-done.1 = bf16[4096,256]{1,0:T(8,128)(2,1)S(1)} copy-done((bf16[4096,256]{1,0:T(8,128)(2,1)S(1)}, bf16[4096,256]{1,0:T(8,128)(2,1)}, u32[]{:S(2)}) %copy-start.1) | copy-done | bytes 2097176
  82.1 1.6 %copy-done.2 = bf16[4096,256]{1,0:T(8,128)(2,1)S(1)} copy-done((bf16[4096,256]{1,0:T(8,128)(2,1)S(1)}, bf16[4096,256]{1,0:T(8,128)(2,1)}, u32[]{:S(2)}) %copy-start.2) | copy-done | bytes 2097176
  83.7 1.6 %copy-done.14 = bf16[4096,256]{1,0:T(8,128)(2,1)S(1)} copy-done((bf16[4096,256]{1,0:T(8,128)(2,1)S(1)}, bf16[4096,256]{1,0:T(8,128)(2,1)}, u32[]{:S(2)}) %copy-start.14) | copy-done | bytes 2097176
  85.3 8.1 %tail_work.1 = (bf16[4096,256]{1,0:T(8,128)(2,1)}, bf16[4096,256]{1,0:T(8,128)(2,1)S(1)}, bf16[32,128,256]{2,1,0:T(8,128)(2,1)S(1)}, f32[576,256]{1,0:T(8,128)S(1)}) custom-call(bf16[4096,256]{1,0:T(8,128)(2,1)S(1)} %copy-done.14, bf16[4096,256]{1,0:T(8,128)(2,1)S(1)} %copy-done.1, bf16[4096,256]{1,0:T(8,128)(2,1)S(1)} %copy-done.2, ...), custom_call_target="tpu_custom_call" | custom-call | flops 10000000000 | bytes 16777216 | tf_op jit(solution)/shard_map/tail_work/pallas_call | solution.py:338
  93.4 1.3 copy-done.10
  94.7 1.3 copy-done.12
  96.3 1.5 collective-permute-done
  97.8 1.7 %collective-permute-start.1 = (f32[144,256]{1,0:T(8,128)S(1)}, f32[144,256]{1,0:T(8,128)S(1)}, u32[]{:S(2)}, u32[]{:S(2)}) collective-permute-start(f32[144,256]{1,0:T(8,128)S(1)} %slice_select_fusion.1), channel_id=1, source_target_pairs={{0,8},{1,9},{2,10},{3,11},{4,12},{5,13},{6,14},{7,15},{8,0},{9,1},... | collective-permute-start | bytes 442376 | tf_op jit(solution)/shard_map/ppermute | solution.py:436
  99.6 6.6 %collective-permute-done.1 = f32[144,256]{1,0:T(8,128)S(1)} collective-permute-done((f32[144,256]{1,0:T(8,128)S(1)}, f32[144,256]{1,0:T(8,128)S(1)}, u32[]{:S(2)}, u32[]{:S(2)}) %collective-permute-start.1) | collective-permute-done | bytes 147488 | tf_op jit(solution)/shard_map/ppermute | solution.py:436
  106.3 1.5 collective-permute-start.2
  107.8 4.4 %collective-permute-done.2 = f32[72,256]{1,0:T(8,128)S(1)} collective-permute-done((f32[72,256]{1,0:T(8,128)S(1)}, f32[72,256]{1,0:T(8,128)S(1)}, u32[]{:S(2)}, u32[]{:S(2)}) %collective-permute-start.2) | collective-permute-done | bytes 73760 | tf_op jit(solution)/shard_map/ppermute | solution.py:436
  112.3 2.2 %collective-permute-start.3 = (f32[72,256]{1,0:T(8,128)S(1)}, f32[72,256]{1,0:T(8,128)S(1)}, u32[]{:S(2)}, u32[]{:S(2)}) collective-permute-start(f32[72,256]{1,0:T(8,128)S(1)} %select_add_fusion.2), channel_id=1, source_target_pairs={{0,2},{1,3},{2,0},{3,1},{4,6},{5,7},{6,4},{7,5},{8,10},{9,11},{10,... | collective-permute-start | bytes 221192 | tf_op jit(solution)/shard_map/ppermute | solution.py:436
  114.5 1.4 collective-permute-start.4
  115.9 1.0 collective-permute-start.5
  117.0 1.6 %copy-done.13 = bf16[32,128,256]{2,1,0:T(8,128)(2,1)S(1)} copy-done((bf16[32,128,256]{2,1,0:T(8,128)(2,1)S(1)}, bf16[32,128,256]{2,1,0:T(8,128)(2,1)}, u32[]{:S(2)}) %copy-start.13) | copy-done | bytes 2097176
  118.6 1.2 copy-done.16
  119.8 3.6 %own_work.1.base = f32[4096,256]{1,0:T(8,128)S(1)} custom-call(s32[64]{0:T(128)S(1)} %copy-done.22, bf16[32,128,128]{2,1,0:T(8,128)(2,1)S(1)} %copy-done.16, bf16[32,128,256]{2,1,0:T(8,128)(2,1)S(1)} %copy-done.13, bf16[4096,256]{1,0:T(8,128)(2,1)S(1)} %copy-done.11, bf16[256,256]{1,0:T(8,128)(2,1)S(1)} %copy-done.4), custom_call_target="tpu_custom_call" | custom-call | flops 10000000000 | bytes 10485760 | tf_op jit(solution)/shard_map/own_work/pallas_call | solution.py:367
  123.4 2.0 %copy-done.8 = f32[4096,256]{1,0:T(8,128)} copy-done((f32[4096,256]{1,0:T(8,128)}, f32[4096,256]{1,0:T(8,128)S(1)}, u32[]{:S(2)}) %copy-start.8) | copy-done | bytes 4194328
  125.4 9.0 %collective-permute-done.4 = f32[72,256]{1,0:T(8,128)S(1)} collective-permute-done((f32[72,256]{1,0:T(8,128)S(1)}, f32[72,256]{1,0:T(8,128)S(1)}, u32[]{:S(2)}, u32[]{:S(2)}) %collective-permute-start.4) | collective-permute-done | bytes 73760 | tf_op jit(solution)/shard_map/ppermute | solution.py:436
  134.5 0.8 broadcast_in_dim.17
  135.3 3.7 %all-to-all-start.2 = ((f32[8,72,256]{2,1,0:T(8,128)}), f32[8,72,256]{2,1,0:T(8,128)S(1)}, u32[]{:S(2)}, u32[]{:S(2)}) async-start(f32[8,72,256]{2,1,0:T(8,128)} %broadcast_in_dim.17), calls=%async_computation.2 | async-start | bytes 1179648 | tf_op jit(solution)/shard_map/all_to_all | solution.py:432
  139.1 2.2 %copy-done.9 = f32[4096,256]{1,0:T(8,128)S(1)} copy-done((f32[4096,256]{1,0:T(8,128)S(1)}, f32[4096,256]{1,0:T(8,128)}, u32[]{:S(2)}) %copy-start.9) | copy-done | bytes 4194328
  141.3 11.0 %scatter_rows.1 = f32[4096,256]{1,0:T(8,128)} custom-call(s32[1,4096]{1,0:T(1,128)S(1)} %bitcast_select_fusion.picks, f32[4096,256]{1,0:T(8,128)S(1)} %copy-done.9, bf16[4096,256]{1,0:T(8,128)(2,1)S(1)} %bitcast.12), custom_call_target="tpu_custom_call" | custom-call | flops 10000000000 | bytes 10485760 | tf_op jit(solution)/shard_map/scatter_rows/pallas_call | solution.py:415
  (55 shorter events, 3.1 us)
Async XLA Ops:
  7.9 7.5 %copy-start = (bf16[4096,256]{1,0:T(8,128)(2,1)S(1)}, bf16[4096,256]{1,0:T(8,128)(2,1)}, u32[]{:S(2)}) copy-start(bf16[4096,256]{1,0:T(8,128)(2,1)} %x.5) | copy-start | bytes 6291460
  7.9 7.5 %copy-start.6 = (s32[1,64]{1,0:T(1,128)S(1)}, s32[1,64]{1,0:T(1,128)}, u32[]{:S(2)}) copy-start(s32[1,64]{1,0:T(1,128)} %src.1) | copy-start | bytes 772
  7.9 7.5 %copy-start.7 = (s32[1,64]{1,0:T(1,128)S(1)}, s32[1,64]{1,0:T(1,128)}, u32[]{:S(2)}) copy-start(s32[1,64]{1,0:T(1,128)} %dst.1) | copy-start | bytes 772
  7.9 57.5 %all-to-all-start = ((bf16[32,128,256]{2,1,0:T(8,128)(2,1)}), bf16[32,128,256]{2,1,0:T(8,128)(2,1)}, u32[]{:S(2)}, u32[]{:S(2)}) async-start(bf16[32,128,256]{2,1,0:T(8,128)(2,1)} %gather_rows.1), calls=%async_computation | async-start | bytes 4194304 | tf_op jit(solution)/shard_map/all_to_all | solution.py:432
  30.6 1.0 copy-start.15
  31.6 1.0 copy-start.17
  32.6 1.0 copy-start.18
  77.5 2.9 %copy-start.3 = (bf16[256,256]{1,0:T(8,128)(2,1)S(1)}, bf16[256,256]{1,0:T(8,128)(2,1)}, u32[]{:S(2)}) copy-start(bf16[256,256]{1,0:T(8,128)(2,1)} %w_neigh.3) | copy-start | bytes 393220
  77.5 2.9 %copy-start.4 = (bf16[256,256]{1,0:T(8,128)(2,1)S(1)}, bf16[256,256]{1,0:T(8,128)(2,1)}, u32[]{:S(2)}) copy-start(bf16[256,256]{1,0:T(8,128)(2,1)} %w_self.5) | copy-start | bytes 393220
  77.5 2.9 %copy-start.5 = (f32[256]{0:T(256)S(1)}, f32[256]{0:T(256)}, u32[]{:S(2)}) copy-start(f32[256]{0:T(256)} %param.18) | copy-start | bytes 3076
  77.6 2.9 %copy-start.20 = (f32[32,8,128]{2,1,0:T(8,128)S(1)}, f32[32,8,128]{2,1,0:T(8,128)}, u32[]{:S(2)}) copy-start(f32[32,8,128]{2,1,0:T(8,128)} %copy-done.19) | copy-start | bytes 393220
  77.6 56.9 %all-to-all-start.1 = ((bf16[32,128,256]{2,1,0:T(8,128)(2,1)}), bf16[32,128,256]{2,1,0:T(8,128)(2,1)S(1)}, u32[]{:S(2)}, u32[]{:S(2)}) async-start(bf16[32,128,256]{2,1,0:T(8,128)(2,1)} %get-tuple-element.30), calls=%async_computation.1 | async-start | bytes 4194304 | tf_op jit(solution)/shard_map/all_to_all | solution.py:432
  80.5 1.6 %copy-start.1 = (bf16[4096,256]{1,0:T(8,128)(2,1)S(1)}, bf16[4096,256]{1,0:T(8,128)(2,1)}, u32[]{:S(2)}) copy-start(bf16[4096,256]{1,0:T(8,128)(2,1)} %x.5) | copy-start | bytes 6291460
  82.1 1.6 %copy-start.2 = (bf16[4096,256]{1,0:T(8,128)(2,1)S(1)}, bf16[4096,256]{1,0:T(8,128)(2,1)}, u32[]{:S(2)}) copy-start(bf16[4096,256]{1,0:T(8,128)(2,1)} %cot.3) | copy-start | bytes 6291460
  83.7 1.6 %copy-start.14 = (bf16[4096,256]{1,0:T(8,128)(2,1)S(1)}, bf16[4096,256]{1,0:T(8,128)(2,1)}, u32[]{:S(2)}) copy-start(bf16[4096,256]{1,0:T(8,128)(2,1)} %get-tuple-element.24.agg) | copy-start | bytes 6291460
  93.4 1.3 copy-start.10
  94.7 1.3 copy-start.12
  96.1 3.5 %copy-start.24 = (s32[1,32]{1,0:T(1,128)S(1)}, s32[1,32]{1,0:T(1,128)}, u32[]{:S(2)}) copy-start(s32[1,32]{1,0:T(1,128)} %counts_in.1) | copy-start | bytes 388
  96.1 11.7 %copy-start.23 = (s32[1,32,128]{2,1,0:T(8,128)S(1)}, s32[1,32,128]{2,1,0:T(8,128)}, u32[]{:S(2)}) copy-start(s32[1,32,128]{2,1,0:T(8,128)} %param.11) | copy-start | bytes 49156
  96.1 20.9 %copy-start.22 = (s32[64]{0:T(128)S(1)}, s32[64]{0:T(128)}, u32[]{:S(2)}) copy-start(s32[64]{0:T(128)} %copy-done.21) | copy-start | bytes 772
  96.1 1.6 %collective-permute-start = (f32[288,256]{1,0:T(8,128)S(1)}, f32[288,256]{1,0:T(8,128)S(1)}, u32[]{:S(2)}, u32[]{:S(2)}) collective-permute-start(f32[288,256]{1,0:T(8,128)S(1)} %slice_select_fusion), channel_id=1, source_target_pairs={{0,1},{1,0},{2,3},{3,2},{4,5},{5,4},{6,7},{7,6},{8,9},{9,8},{10,11... | collective-permute-start | bytes 884744 | tf_op jit(solution)/shard_map/ppermute | solution.py:436
  96.3 20.7 %copy-start.11 = (bf16[4096,256]{1,0:T(8,128)(2,1)S(1)}, bf16[4096,256]{1,0:T(8,128)(2,1)}, u32[]{:S(2)}) copy-start(bf16[4096,256]{1,0:T(8,128)(2,1)} %copy-done.10) | copy-start | bytes 6291460
  97.8 8.4 %collective-permute-start.1 = (f32[144,256]{1,0:T(8,128)S(1)}, f32[144,256]{1,0:T(8,128)S(1)}, u32[]{:S(2)}, u32[]{:S(2)}) collective-permute-start(f32[144,256]{1,0:T(8,128)S(1)} %slice_select_fusion.1), channel_id=1, source_target_pairs={{0,8},{1,9},{2,10},{3,11},{4,12},{5,13},{6,14},{7,15},{8,0},{9,1},... | collective-permute-start | bytes 442376 | tf_op jit(solution)/shard_map/ppermute | solution.py:436
  106.3 5.9 %collective-permute-start.2 = (f32[72,256]{1,0:T(8,128)S(1)}, f32[72,256]{1,0:T(8,128)S(1)}, u32[]{:S(2)}, u32[]{:S(2)}) collective-permute-start(f32[72,256]{1,0:T(8,128)S(1)} %slice_select_fusion.2), channel_id=1, source_target_pairs={{0,16},{1,17},{2,18},{3,19},{4,20},{5,21},{6,22},{7,23},{8,24},{9,... | collective-permute-start | bytes 221192 | tf_op jit(solution)/shard_map/ppermute | solution.py:436
  112.3 13.2 %collective-permute-start.3 = (f32[72,256]{1,0:T(8,128)S(1)}, f32[72,256]{1,0:T(8,128)S(1)}, u32[]{:S(2)}, u32[]{:S(2)}) collective-permute-start(f32[72,256]{1,0:T(8,128)S(1)} %select_add_fusion.2), channel_id=1, source_target_pairs={{0,2},{1,3},{2,0},{3,1},{4,6},{5,7},{6,4},{7,5},{8,10},{9,11},{10,... | collective-permute-start | bytes 221192 | tf_op jit(solution)/shard_map/ppermute | solution.py:436
  114.5 19.9 %collective-permute-start.4 = (f32[72,256]{1,0:T(8,128)S(1)}, f32[72,256]{1,0:T(8,128)S(1)}, u32[]{:S(2)}, u32[]{:S(2)}) collective-permute-start(f32[72,256]{1,0:T(8,128)S(1)} %select_add_fusion.2), channel_id=1, source_target_pairs={{0,4},{1,5},{2,6},{3,7},{4,0},{5,1},{6,2},{7,3},{8,12},{9,13},{10,... | collective-permute-start | bytes 221192 | tf_op jit(solution)/shard_map/ppermute | solution.py:436
  115.9 18.5 %collective-permute-start.5 = (f32[72,256]{1,0:T(8,128)S(1)}, f32[72,256]{1,0:T(8,128)S(1)}, u32[]{:S(2)}, u32[]{:S(2)}) collective-permute-start(f32[72,256]{1,0:T(8,128)S(1)} %select_add_fusion.2), channel_id=1, source_target_pairs={{0,6},{1,7},{2,4},{3,5},{4,2},{5,3},{6,0},{7,1},{8,14},{9,15},{10,... | collective-permute-start | bytes 221192 | tf_op jit(solution)/shard_map/ppermute | solution.py:436
  117.0 1.6 %copy-start.13 = (bf16[32,128,256]{2,1,0:T(8,128)(2,1)S(1)}, bf16[32,128,256]{2,1,0:T(8,128)(2,1)}, u32[]{:S(2)}) copy-start(bf16[32,128,256]{2,1,0:T(8,128)(2,1)} %copy-done.12) | copy-start | bytes 6291460
  118.6 1.2 copy-start.16
  123.4 2.0 %copy-start.8 = (f32[4096,256]{1,0:T(8,128)}, f32[4096,256]{1,0:T(8,128)S(1)}, u32[]{:S(2)}) copy-start(f32[4096,256]{1,0:T(8,128)S(1)} %own_work.1.base) | copy-start | bytes 12582916
  135.3 16.9 %all-to-all-start.2 = ((f32[8,72,256]{2,1,0:T(8,128)}), f32[8,72,256]{2,1,0:T(8,128)S(1)}, u32[]{:S(2)}, u32[]{:S(2)}) async-start(f32[8,72,256]{2,1,0:T(8,128)} %broadcast_in_dim.17), calls=%async_computation.2 | async-start | bytes 1179648 | tf_op jit(solution)/shard_map/all_to_all | solution.py:432
  139.1 2.2 %copy-start.9 = (f32[4096,256]{1,0:T(8,128)S(1)}, f32[4096,256]{1,0:T(8,128)}, u32[]{:S(2)}) copy-start(f32[4096,256]{1,0:T(8,128)} %copy-done.8) | copy-start | bytes 12582916
  (2 other events, 1.2 us)

commit v2 on v1

v2 whole, which is shorter than its diff:
```python
import functools

import jax
import jax.numpy as jnp
from jax import lax
from jax.experimental import pallas as pl
from jax.experimental.pallas import tpu as pltpu
from jax.sharding import PartitionSpec as P

AXES = ("row", "col")
LANES = 128
MIDDLE_MIB = 52
SCATTER_MIB = 52
VMEM = pl.BlockSpec(memory_space=pltpu.VMEM)
SMEM = pl.BlockSpec(memory_space=pltpu.SMEM)
ANY = pl.BlockSpec(memory_space=pl.ANY)
F32 = jnp.float32
BF16 = jnp.bfloat16


def matmul(a, b):
    return jnp.dot(a, b, preferred_element_type=F32)


def matmul_t(a, b):
    return lax.dot_general(a, b, (((1,), (1,)), ((), ())), preferred_element_type=F32)


def params(mib):
    return pltpu.CompilerParams(vmem_limit_bytes=int(mib * 1024 * 1024))


def cost(flops, nbytes):
    return pl.CostEstimate(flops=int(flops), bytes_accessed=int(nbytes), transcendentals=0)


def loosen(target, first, value):
    rows, width = value.shape
    halves = width // LANES
    for h in range(halves):
        at = pl.ds(first * halves + h, rows, stride=halves)
        target[at, :] = value[:, h * LANES : (h + 1) * LANES].astype(F32)


def tighten(source, first, rows, halves):
    parts = [source[pl.ds(first * halves + h, rows, stride=halves), :] for h in range(halves)]
    return jnp.concatenate(parts, 1)


def row_at(index, halves):
    return pl.ds(pl.multiple_of(index * halves, halves), halves)


def gather_kernel(picks_in, counts_in, x_in, out_in, picks, counts, x, out, wide, stage, sems):
    rows, width = x.shape
    peers, slots = picks.shape
    halves = width // LANES
    parts = 4
    chunk = rows // parts
    step = 128
    copies = [
        pltpu.make_async_copy(picks_in, picks, sems.at[0]),
        pltpu.make_async_copy(counts_in, counts, sems.at[1]),
    ]
    for c in range(parts):
        at = pl.ds(c * chunk, chunk)
        copies.append(pltpu.make_async_copy(x_in.at[at], x.at[at], sems.at[2 + c]))
    for copy in copies:
        copy.start()
    for c in range(parts):
        copies[2 + c].wait()

        @pl.loop(c * chunk // step, (c + 1) * chunk // step)
        def _(i):
            first = pl.multiple_of(i * step, step)
            loosen(wide, first, x[pl.ds(first, step), :])

    copies[0].wait()
    copies[1].wait()

    @pl.loop(0, peers)
    def _(p):
        for k in range(slots):
            stage[row_at(k, halves), :] = wide[row_at(picks[p, k], halves), :]
        used = lax.broadcasted_iota(jnp.int32, (slots, width), 0) < counts[0, p]
        out[p] = jnp.where(used, tighten(stage, 0, slots, halves), 0.0).astype(BF16)
        pltpu.make_async_copy(out.at[p], out_in.at[p], sems.at[2 + parts]).start()

    pltpu.make_async_copy(out, out_in, sems.at[2 + parts]).wait()


def gather_rows(x, picks, counts):
    rows, width = x.shape
    peers, slots = picks.shape
    halves = width // LANES
    return pl.pallas_call(
        gather_kernel,
        out_shape=jax.ShapeDtypeStruct((peers, slots, width), BF16),
        in_specs=[ANY, ANY, ANY],
        out_specs=ANY,
        scratch_shapes=[
            pltpu.SMEM(picks.shape, jnp.int32),
            pltpu.SMEM(counts.shape, jnp.int32),
            pltpu.VMEM((rows, width), BF16),
            pltpu.VMEM((peers, slots, width), BF16),
            pltpu.VMEM((rows * halves, LANES), F32),
            pltpu.VMEM((slots * halves, LANES), F32),
            pltpu.SemaphoreType.DMA((7,)),
        ],
        compiler_params=params(60),
        cost_estimate=cost(1e10, 4 * rows * width),
        name="gather_rows",
    )(picks, counts, x)


def local_kernel(src, dst, tiles, adj, edge_t, own_t, by_src, scale, order):
    count, tb, _ = tiles.shape
    own = own_t.shape[0]

    @pl.loop(0, count)
    def _(t):
        order[src[0, t]] = t

    scale[...] = jnp.zeros_like(scale)
    ones = jnp.ones((8, tb), BF16)

    def take(s, turned):
        t = order[s]
        d = dst[0, t]
        by_src[s] = d
        tile = tiles[t].astype(F32)
        straight = tile.astype(BF16)
        adj[s] = straight
        turned(tile.T.astype(BF16))
        scale[d] += matmul_t(ones, straight)

    @pl.loop(0, own, unroll=4)
    def _(s):
        def keep(value):
            own_t[s] = value

        take(s, keep)

    @pl.loop(own, count, unroll=4)
    def _(s):
        def keep(value):
            edge_t[s - own] = value

        take(s, keep)

    scale[...] = 1.0 / (1.0 + scale[...])


def local_work(src, dst, tiles, own):
    count, tb, _ = tiles.shape
    edges = count - own
    return pl.pallas_call(
        local_kernel,
        out_shape=(
            jax.ShapeDtypeStruct((count, tb, tb), BF16),
            jax.ShapeDtypeStruct((edges, tb, tb), BF16),
            jax.ShapeDtypeStruct((own, tb, tb), BF16),
            jax.ShapeDtypeStruct((count,), jnp.int32),
            jax.ShapeDtypeStruct((own, 8, tb), F32),
        ),
        in_specs=[SMEM, SMEM, VMEM],
        out_specs=(VMEM, VMEM, VMEM, SMEM, VMEM),
        scratch_shapes=[pltpu.SMEM((count,), jnp.int32)],
        compiler_params=params(48),
        cost_estimate=cost(2e10, 4 * tiles.size),
        name="local_work",
    )(src, dst, tiles)


def spread_scale(scale, scale_v):
    own, _, tb = scale.shape

    @pl.loop(0, own, unroll=4)
    def _(s):
        scale_v[s] = jnp.broadcast_to(scale[s, 0:1, :], (tb, tb)).T


def rates_of(scale_v, which, size, width):
    rate = scale_v[which].reshape(size, scale_v.shape[2])
    return jnp.concatenate([rate] * (width // scale_v.shape[2]), 1)


def activation(x, agg, cot, w_self, w_neigh, bias):
    pre = matmul(x, w_self) + matmul(agg, w_neigh) + bias
    sig = 0.5 * jnp.tanh(0.5 * pre) + 0.5
    dpre = cot.astype(F32) * (sig * (1.0 + pre * (1.0 - sig)))
    return pre * sig, dpre


def middle_kernel(
    by_src, arrived, adj, edge_t, x, cot, scale, w_self, w_neigh, bias,
    agg_out, back_out,
    arrived_v, adj_v, edge_tv, acc, scale_v, x_v, cot_v, agg_v, g_v, back_v, sems,
):
    own, tb, width = acc.shape
    edges = edge_tv.shape[0]
    rows = own * tb
    parts = 4
    number = iter(range(sems.shape[0]))

    def start(source, target):
        copy = pltpu.make_async_copy(source, target, sems.at[next(number)])
        copy.start()
        return copy

    def cuts(size):
        return [pl.ds(c * (size // parts), size // parts) for c in range(parts)]

    def start_cuts(source, target, size):
        return [start(source.at[at], target.at[at]) for at in cuts(size)]

    coming = []
    for first, size, source, target in ((own, edges, arrived, arrived_v), (0, own, x, x_v)):
        each = size // parts
        unit = target.shape[0] // parts
        for c in range(parts):
            tiles = pl.ds(first + c * each, each)
            at = pl.ds(c * unit, unit)
            needs = start(adj.at[tiles], adj_v.at[tiles]), start(source.at[at], target.at[at])
            coming.append((first + c * each, each, needs))
    cots = start_cuts(cot, cot_v, rows)
    in_edge_t = start(edge_t, edge_tv)
    acc[...] = jnp.zeros_like(acc)
    spread_scale(scale, scale_v)

    for first, each, needs in coming:
        for copy in needs:
            copy.wait()

        @pl.loop(0, each, unroll=8)
        def _(i):
            s = first + i
            if first < own:
                block = x_v[pl.ds(pl.multiple_of(s * tb, tb), tb), :]
            else:
                block = arrived_v[s - own]
            acc[by_src[s]] += matmul(adj_v[s], block)

    each = edges // parts
    block = min(8, own // parts)
    size = block * tb
    leaving = []
    for c in range(parts):
        cots[c].wait()

        @pl.loop(c * (own // parts) // block, (c + 1) * (own // parts) // block)
        def _(i):
            at = pl.ds(pl.multiple_of(i * size, size), size)
            which = pl.ds(i * block, block)
            rate = rates_of(scale_v, which, size, width)
            agg = (acc[which].reshape(size, width) * rate).astype(BF16)
            agg_v[at, :] = agg
            _, dpre = activation(
                x_v[at, :], agg, cot_v[at, :], w_self[...], w_neigh[...], bias[...]
            )
            g = (matmul_t(dpre.astype(BF16), w_neigh[...]) * rate).astype(BF16)
            g_v[which] = g.reshape(block, tb, width)

        at = cuts(rows)[c]
        leaving.append(start(agg_v.at[at], agg_out.at[at]))

    in_edge_t.wait()
    for c in range(parts):

        @pl.loop(c * each, (c + 1) * each, unroll=8)
        def _(s):
            back_v[s] = matmul(edge_tv[s], g_v[by_src[own + s]]).astype(BF16)

        at = cuts(edges)[c]
        leaving.append(start(back_v.at[at], back_out.at[at]))
    for copy in leaving:
        copy.wait()


def middle_work(by_src, arrived, adj, edge_t, x, cot, scale, w_self, w_neigh, bias):
    edges, tb, width = arrived.shape
    own = scale.shape[0]
    rows, hidden = cot.shape
    return pl.pallas_call(
        middle_kernel,
        out_shape=(
            jax.ShapeDtypeStruct((rows, width), BF16),
            jax.ShapeDtypeStruct((edges, tb, width), BF16),
        ),
        in_specs=[SMEM] + [ANY] * 5 + [VMEM] * 4,
        out_specs=(ANY, ANY),
        scratch_shapes=[
            pltpu.VMEM((edges, tb, width), BF16),
            pltpu.VMEM((own + edges, tb, tb), BF16),
            pltpu.VMEM((edges, tb, tb), BF16),
            pltpu.VMEM((own, tb, width), F32),
            pltpu.VMEM((own, tb, tb), F32),
            pltpu.VMEM((rows, width), BF16),
            pltpu.VMEM((rows, hidden), BF16),
            pltpu.VMEM((rows, width), BF16),
            pltpu.VMEM((own, tb, width), BF16),
            pltpu.VMEM((edges, tb, width), BF16),
            pltpu.SemaphoreType.DMA((32,)),
        ],
        compiler_params=params(MIDDLE_MIB),
        cost_estimate=cost(2e10, 16 * rows * width),
        name="middle_work",
    )(by_src, arrived, adj, edge_t, x, cot, scale, w_self, w_neigh, bias)


def tail_kernel(
    agg_in, x_in, cot_in, scale, w_self, w_neigh, bias,
    layer_out, dpre_out, g_out, terms,
    agg, x, cot, layer_v, dpre_v, g_v, scale_v, sems,
):
    rows, width = x.shape
    own, tb, _ = g_v.shape
    hidden = cot.shape[1]
    block = 4
    size = block * tb
    steps = own // block
    sources = ((agg_in, agg), (x_in, x), (cot_in, cot))

    def at_step(i):
        return pl.ds(i * size, size), pl.ds(i * block, block)

    def fetch(i):
        at, _ = at_step(i)
        return [
            pltpu.make_async_copy(source.at[at], target.at[at], sems.at[3 * i + n])
            for n, (source, target) in enumerate(sources)
        ]

    for i in range(steps):
        for copy in fetch(i):
            copy.start()
    spread_scale(scale, scale_v)
    terms[...] = jnp.zeros_like(terms)
    leaving = []
    for i in range(steps):
        at, which = at_step(i)
        for copy in fetch(i):
            copy.wait()
        near = agg[at, :]
        layer, dpre = activation(
            x[at, :], near, cot[at, :], w_self[...], w_neigh[...], bias[...]
        )
        layer_v[at, :] = layer.astype(BF16)
        dpre_b = dpre.astype(BF16)
        dpre_v[at, :] = dpre_b
        rate = rates_of(scale_v, which, size, width)
        g = (matmul_t(dpre_b, w_neigh[...]) * rate).astype(BF16)
        g_v[which] = g.reshape(block, tb, width)
        dims = (((0,), (0,)), ((), ()))
        terms[:width, :] += lax.dot_general(x[at, :], dpre_b, dims, preferred_element_type=F32)
        terms[width : 2 * width, :] += lax.dot_general(
            near, dpre_b, dims, preferred_element_type=F32
        )
        terms[2 * width : 2 * width + 8, :] += jnp.sum(dpre.reshape(size // 8, 8, hidden), axis=0)
        for n, (source, target) in enumerate(
            (
                (layer_v.at[at], layer_out.at[at]),
                (dpre_v.at[at], dpre_out.at[at]),
                (g_v.at[which], g_out.at[which]),
            )
        ):
            copy = pltpu.make_async_copy(source, target, sems.at[3 * (steps + i) + n])
            copy.start()
            leaving.append(copy)
    for copy in leaving:
        copy.wait()


def tail_work(agg, x, cot, scale, w_self, w_neigh, bias, spare):
    rows, width = x.shape
    own, _, tb = scale.shape
    hidden = cot.shape[1]
    return pl.pallas_call(
        tail_kernel,
        out_shape=(
            jax.ShapeDtypeStruct((rows, hidden), BF16),
            jax.ShapeDtypeStruct((rows, hidden), BF16),
            jax.ShapeDtypeStruct((own, tb, width), BF16),
            jax.ShapeDtypeStruct((2 * width + spare, hidden), F32),
        ),
        in_specs=[ANY] * 3 + [VMEM] * 4,
        out_specs=(ANY, ANY, ANY, VMEM),
        scratch_shapes=[
            pltpu.VMEM((rows, width), BF16),
            pltpu.VMEM((rows, width), BF16),
            pltpu.VMEM((rows, hidden), BF16),
            pltpu.VMEM((rows, hidden), BF16),
            pltpu.VMEM((rows, hidden), BF16),
            pltpu.VMEM((own, tb, width), BF16),
            pltpu.VMEM((own, tb, tb), F32),
            pltpu.SemaphoreType.DMA((6 * (own // 4),)),
        ],
        compiler_params=params(62.5),
        cost_estimate=cost(1e10, 16 * rows * width),
        name="tail_work",
    )(agg, x, cot, scale, w_self, w_neigh, bias)


def own_kernel(by_src, own_t, g, dpre_b, w_self, out):
    own, tb, width = g.shape

    @pl.loop(0, own, unroll=4)
    def _(s):
        at = pl.ds(pl.multiple_of(s * tb, tb), tb)
        back = matmul(own_t[s], g[by_src[s]])
        out[at, :] = back + matmul_t(dpre_b[at, :], w_self[...])


def own_work(by_src, own_t, g, dpre_b, w_self):
    own, tb, width = g.shape
    return pl.pallas_call(
        own_kernel,
        out_shape=jax.ShapeDtypeStruct((own * tb, width), F32),
        in_specs=[SMEM] + [VMEM] * 4,
        out_specs=VMEM,
        compiler_params=params(24),
        cost_estimate=cost(1e10, 10 * own * tb * width),
        name="own_work",
    )(by_src, own_t, g, dpre_b, w_self)


def scatter_kernel(
    targets_in, base_in, returned_in, out_in, targets, base, returned, out, stage, sems, *sums
):
    rows, width = base.shape
    peers, slots = targets.shape
    halves = width // LANES
    copies = [
        pltpu.make_async_copy(targets_in, targets, sems.at[0]),
        pltpu.make_async_copy(base_in, base, sems.at[1]),
    ]
    parts = 4
    each = peers // parts
    for c in range(parts):
        at = pl.ds(c * each, each)
        copies.append(pltpu.make_async_copy(returned_in.at[at], returned.at[at], sems.at[3 + c]))
    copies.append(copies.pop(1))
    for copy in copies:
        copy.start()
    for total in sums:
        total[...] = jnp.zeros_like(total)
    copies[0].wait()

    for c in range(parts):
        copies[1 + c].wait()

        @pl.loop(c * each, (c + 1) * each)
        def _(p):
            loosen(stage, 0, returned[p])
            for k in range(0, slots, len(sums)):
                places = [row_at(targets[p, k + j], halves) for j in range(len(sums))]
                values = [
                    total[place, :] + stage[row_at(k + j, halves), :]
                    for j, (total, place) in enumerate(zip(sums, places))
                ]
                for total, place, value in zip(sums, places, values):
                    total[place, :] = value

    copies[1 + parts].wait()
    block = 256

    @pl.loop(0, rows // block)
    def _(i):
        first = pl.multiple_of(i * block, block)
        at = pl.ds(first, block)
        value = base[at, :]
        for total in sums:
            value += tighten(total, first, block, halves)
        out[at, :] = value
        pltpu.make_async_copy(out.at[at], out_in.at[at], sems.at[2]).start()

    pltpu.make_async_copy(out, out_in, sems.at[2]).wait()


def scatter_rows(targets, base, returned):
    rows, width = base.shape
    peers, slots = targets.shape
    halves = width // LANES
    return pl.pallas_call(
        scatter_kernel,
        out_shape=jax.ShapeDtypeStruct((rows, width), F32),
        in_specs=[ANY, ANY, ANY],
        out_specs=ANY,
        scratch_shapes=[
            pltpu.SMEM(targets.shape, jnp.int32),
            pltpu.VMEM((rows, width), F32),
            pltpu.VMEM((peers, slots, width), BF16),
            pltpu.VMEM((rows, width), F32),
            pltpu.VMEM((slots * halves, LANES), F32),
            pltpu.SemaphoreType.DMA((7,)),
        ]
        + [pltpu.VMEM(((rows + 8) * halves, LANES), F32)] * 4,
        compiler_params=params(SCATTER_MIB),
        cost_estimate=cost(1e10, 10 * rows * width),
        name="scatter_rows",
    )(targets, base, returned)


def exchange(block, groups=None):
    return lax.all_to_all(block, AXES, 0, 0, tiled=True, axis_index_groups=groups)


def flip(value, bit, members):
    return lax.ppermute(value, AXES, [(i, i ^ bit) for i in range(members)])


def split_bits(shape):
    n_row, n_col = shape
    inner = n_col // 4 if n_col % 4 == 0 else n_col
    near = [1 << i for i in range(inner.bit_length() - 1)]
    near += [n_col << i for i in range(n_row.bit_length() - 1)]
    return near, [inner << i for i in range((n_col // inner).bit_length() - 1)]


def share_of_total(terms, shape):
    members = shape[0] * shape[1]
    near, far = split_bits(shape)
    me = lax.axis_index(AXES)
    for bit in near:
        upper = (me & bit) != 0
        half = terms.shape[0] // 2
        low, high = terms[:half], terms[half:]
        terms = jnp.where(upper, high, low) + flip(jnp.where(upper, low, high), bit, members)
    for bit in far:
        terms = terms + flip(terms, bit, members)
    return terms


def share_groups(shape):
    members = shape[0] * shape[1]
    near, _ = split_bits(shape)

    def place(device):
        return sum(1 << (len(near) - 1 - i) for i, bit in enumerate(near) if device & bit)

    mask = sum(near)
    planes = {}
    for device in range(members):
        planes.setdefault(device & ~mask, []).append(device)
    groups = [sorted(plane, key=place) for _, plane in sorted(planes.items())]
    return groups


def on_device(
    shape, features, send_rows, counts, tile_dst, tile_src, tiles, w_self, w_neigh, bias, cotangent
):
    rows, width = features.shape
    peers, slots = send_rows.shape[1:]
    picks = send_rows[0]
    outgoing = gather_rows(features, picks, counts)
    arrived = exchange(outgoing)
    adj, edge_t, own_t, by_src, scale = local_work(tile_src, tile_dst, tiles[0], rows // slots)
    keep = jnp.arange(slots, dtype=jnp.int32)[None, :] < counts[0][:, None]
    targets = jnp.where(keep, picks, rows)
    agg, back_b = middle_work(
        by_src, arrived, adj, edge_t, features, cotangent, scale, w_self, w_neigh, bias[None]
    )
    returned = exchange(back_b)
    spare = 8 << len(split_bits(shape)[0])
    layer_out, dpre_b, g, terms = tail_work(
        agg, features, cotangent, scale, w_self, w_neigh, bias[None], spare
    )
    own_grad = own_work(by_src, own_t, g, dpre_b, w_self)
    inv_root = 1.0 / jnp.sqrt(F32(rows * shape[0] * shape[1]))
    share = share_of_total(terms, shape) * inv_root
    groups = share_groups(shape)
    packed = jnp.broadcast_to(share[None], (len(groups[0]),) + share.shape)
    packed, returned = lax.optimization_barrier((packed, returned))
    terms = exchange(packed, groups).reshape(terms.shape)
    grad_features = scatter_rows(targets, own_grad, returned)
    grad_bias = jnp.sum(terms[2 * width : 2 * width + 8], axis=0)
    return layer_out, grad_features, terms[:width], terms[width : 2 * width], grad_bias


def solution(mesh):
    both = P(AXES)
    in_specs = (both,) * 6 + (P(),) * 3 + (both,)
    out_specs = (both, both, P(), P(), P())
    shape = (mesh.shape["row"], mesh.shape["col"])
    return jax.shard_map(
        functools.partial(on_device, shape),
        mesh=mesh,
        in_specs=in_specs,
        out_specs=out_specs,
        check_vma=False,
    )
```

time: 154 us -> 147 us (0.955)
  local copies, waits for them, and re-layouts: 19.5 us -> 6.59 us
  Pallas kernels: 57.3 us -> 46 us
  waiting for transfers between devices: 52.2 us -> 62.2 us
  other arithmetic: 1.71 us -> 7.33 us
  starting transfers between devices: 22.1 us -> 23.7 us
    unnamed x50 -> x26, local copies, waits for them, and re-layouts: 18.6 us -> 4.9 us
    all_to_all x3, waiting for transfers between devices: 30.7 us -> 43.2 us  [exchange(): lax.all_to_all(block, AXES, 0, 0, tiled=True, axis_index_groups=groups)]
    pallas_call x1, Pallas kernels: 15.1 us -> 6.32 us  [local_work(): pl.pallas_call(local_kernel, out_shape=(jax.ShapeDtypeStruct((count, tb,...]
    select_n x3, other arithmetic: 0.07 us -> 3.64 us  [share_of_total(): jnp.where(upper, low, high)]
    add x3, other arithmetic: 0.1 us -> 3.02 us  [share_of_total(): jnp.where(upper, high, low)]
    ppermute x6 -> x5, waiting for transfers between devices: 21.6 us -> 19 us  [flip(): return lax.ppermute(value, AXES, [(i, i ^ bit) for i in range(members)])]
    pallas_call x1, Pallas kernels: 11 us -> 8.89 us  [scatter_rows(): pl.pallas_call(scatter_kernel, out_shape=jax.ShapeDtypeStruct((rows, widt...]
    pallas_call x1, Pallas kernels: 12.1 us -> 10.2 us  [middle_work(): pl.pallas_call(middle_kernel, out_shape=(jax.ShapeDtypeStruct((rows, widt...]
  transfers between devices with their start and end apart: 9 -> 8, of which waited for: 5 -> 7; matrix products, arithmetic and copies ran while one was open for 0% -> 5% of each run, Pallas kernels for 25% -> 20%
where the time goes in v2:
time: 147 us
  waiting for transfers between devices  62.2 us (42%)
  Pallas kernels  46 us (31%)
  starting transfers between devices  23.7 us (16%)
  other arithmetic  7.33 us (5%)
  local copies, waits for them, and re-layouts  6.59 us (4%)
    all_to_all x3, waiting for transfers between devices, exchange(): lax.all_to_all(block, AXES, 0, 0, tiled=True, axis_index_groups=groups)  43.2 us
    ppermute x5, waiting for transfers between devices, flip(): return lax.ppermute(value, AXES, [(i, i ^ bit) for i in range(members)])  19 us
    all_to_all x3, starting transfers between devices, exchange(): lax.all_to_all(block, AXES, 0, 0, tiled=True, axis_index_groups=groups)  14.9 us
    pallas_call x1, Pallas kernels, middle_work(): pl.pallas_call(middle_kernel, out_shape=(jax.ShapeDtypeStruct((rows, widt...  10.2 us
    pallas_call x1, Pallas kernels, tail_work(): pl.pallas_call(tail_kernel, out_shape=(jax.ShapeDtypeStruct((rows, hidden...  9.7 us
    pallas_call x1, Pallas kernels, scatter_rows(): pl.pallas_call(scatter_kernel, out_shape=jax.ShapeDtypeStruct((rows, widt...  8.89 us
    ppermute x5, starting transfers between devices, flip(): return lax.ppermute(value, AXES, [(i, i ^ bit) for i in range(members)])  8.81 us
    pallas_call x1, Pallas kernels, gather_rows(): pl.pallas_call(gather_kernel, out_shape=jax.ShapeDtypeStruct((peers, slot...  7.12 us
  transfers between devices with their start and end apart: 8, of which 7 were waited for; matrix products, arithmetic and copies ran while one was open for 5% of the time, Pallas kernels for 20%

profile of v2, /device:TPU:0, one launch (start us, length us, event | category | flops | bytes accessed | tf_op | source)
XLA Modules:
  0.0 146.7 jit_solution(3853010645100125928)
XLA Ops:
  0.6 7.1 %gather_rows.1 = bf16[32,128,256]{2,1,0:T(8,128)(2,1)} custom-call(s32[32,128]{1,0:T(8,128)} %bitcast.10, s32[1,32]{1,0:T(1,128)} %counts_in.1, bf16[4096,256]{1,0:T(8,128)(2,1)} %x_in.3), custom_call_target="tpu_custom_call" | custom-call | flops 10000000000 | bytes 4194304 | tf_op jit(solution)/shard_map/gather_rows/pallas_call | solution.py:96
  7.8 7.5 %all-to-all-start = ((bf16[32,128,256]{2,1,0:T(8,128)(2,1)}), bf16[32,128,256]{2,1,0:T(8,128)(2,1)}, u32[]{:S(2)}, u32[]{:S(2)}) async-start(bf16[32,128,256]{2,1,0:T(8,128)(2,1)} %gather_rows.1), calls=%async_computation | async-start | bytes 4194304 | tf_op jit(solution)/shard_map/all_to_all | solution.py:505
  15.3 0.0 copy-start
  15.3 6.3 %local_work.1 = (bf16[64,128,128]{2,1,0:T(8,128)(2,1)S(1)}, bf16[32,128,128]{2,1,0:T(8,128)(2,1)S(1)}, bf16[32,128,128]{2,1,0:T(8,128)(2,1)S(1)}, s32[64]{0:T(128)S(1)}, f32[32,8,128]{2,1,0:T(8,128)S(1)}) custom-call(s32[1,64]{1,0:T(1,128)S(1)} %copy-done.4, s32[1,64]{1,0:T(1,128)S(1)} %copy-done.5, s32[64,128,128]{2,1,0:T(8,128)} %bitcast.12), custom_call_target="tpu_custom_call" | custom-call | flops 20000000000 | bytes 4194304 | tf_op jit(solution)/shard_map/local_work/pallas_call | solution.py:157
  21.7 1.3 copy-done.9
  23.0 42.3 %all-to-all-done.arrived = bf16[32,128,256]{2,1,0:T(8,128)(2,1)} async-done(((bf16[32,128,256]{2,1,0:T(8,128)(2,1)}), bf16[32,128,256]{2,1,0:T(8,128)(2,1)}, u32[]{:S(2)}, u32[]{:S(2)}) %all-to-all-start) | async-done | bytes 2097184 | tf_op jit(solution)/shard_map/all_to_all | solution.py:505
  65.3 10.2 %middle_work.1 = (bf16[4096,256]{1,0:T(8,128)(2,1)}, bf16[32,128,256]{2,1,0:T(8,128)(2,1)}) custom-call(s32[64]{0:T(128)S(1)} %get-tuple-element.18.by_src, bf16[32,128,256]{2,1,0:T(8,128)(2,1)} %all-to-all-done.arrived, bf16[64,128,128]{2,1,0:T(8,128)(2,1)} %copy-done.9, bf16[32,128,128]{2,1,0:T(8,128)(2,1)S(1)} %get-tuple-element.20.edge_t, ...), custom_call_target="tpu_custom_call" | custom-call | flops 20000000000 | bytes 16777216 | tf_op jit(solution)/shard_map/middle_work/pallas_call | solution.py:284
  75.5 3.7 %all-to-all-start.1 = ((bf16[32,128,256]{2,1,0:T(8,128)(2,1)}), bf16[32,128,256]{2,1,0:T(8,128)(2,1)}, u32[]{:S(2)}, u32[]{:S(2)}) async-start(bf16[32,128,256]{2,1,0:T(8,128)(2,1)} %get-tuple-element.28), calls=%async_computation.1 | async-start | bytes 4194304 | tf_op jit(solution)/shard_map/all_to_all | solution.py:505
  79.2 9.7 %tail_work.1 = (bf16[4096,256]{1,0:T(8,128)(2,1)}, bf16[4096,256]{1,0:T(8,128)(2,1)}, bf16[32,128,256]{2,1,0:T(8,128)(2,1)}, f32[576,256]{1,0:T(8,128)}) custom-call(bf16[4096,256]{1,0:T(8,128)(2,1)} %get-tuple-element.22.agg_in, bf16[4096,256]{1,0:T(8,128)(2,1)} %x_in.3, bf16[4096,256]{1,0:T(8,128)(2,1)} %cot_in.1, f32[32,8,128]{2,1,0:T(8,128)} %copy-done.10, ...), custom_call_target="tpu_custom_call" | custom-call | flops 10000000000 | bytes 16777216 | tf_op jit(solution)/shard_map/tail_work/pallas_call | solution.py:378
  89.0 2.0 %slice_select_fusion = f32[288,256]{1,0:T(8,128)} fusion(f32[576,256]{1,0:T(8,128)} %get-tuple-element.27, pred[]{:T(512)S(6)} %ne.11), kind=kLoop, calls=%fused_computation.1 | loop fusion | flops 73728 | bytes 884737 | tf_op jit(solution)/shard_map/jit(_where)/select_n | solution.py:528
  90.9 1.9 %collective-permute-done = f32[288,256]{1,0:T(8,128)} collective-permute-done((f32[288,256]{1,0:T(8,128)}, f32[288,256]{1,0:T(8,128)}, u32[]{:S(2)}, u32[]{:S(2)}) %collective-permute-start) | collective-permute-done | bytes 294944 | tf_op jit(solution)/shard_map/ppermute | solution.py:509
  92.9 1.9 %select_add_fusion = f32[288,256]{1,0:T(8,128)} fusion(f32[288,256]{1,0:T(8,128)} %collective-permute-done, f32[576,256]{1,0:T(8,128)} %get-tuple-element.27, pred[]{:T(512)S(6)} %ne.11), kind=kLoop, calls=%fused_computation | loop fusion | flops 147456 | bytes 1179649 | tf_op jit(solution)/shard_map/add | solution.py:528
  94.8 1.7 %slice_select_fusion.1 = f32[144,256]{1,0:T(8,128)} fusion(f32[288,256]{1,0:T(8,128)} %select_add_fusion, pred[]{:T(512)S(6)} %ne.10), kind=kLoop, calls=%fused_computation.3 | loop fusion | flops 36864 | bytes 442369 | tf_op jit(solution)/shard_map/jit(_where)/select_n | solution.py:528
  96.4 1.4 collective-permute-start.1
  97.8 6.8 %collective-permute-done.1 = f32[144,256]{1,0:T(8,128)} collective-permute-done((f32[144,256]{1,0:T(8,128)}, f32[144,256]{1,0:T(8,128)}, u32[]{:S(2)}, u32[]{:S(2)}) %collective-permute-start.1) | collective-permute-done | bytes 147488 | tf_op jit(solution)/shard_map/ppermute | solution.py:509
  104.7 1.1 select_add_fusion.1
  105.8 1.6 %collective-permute-start.2 = (f32[72,256]{1,0:T(8,128)S(1)}, f32[72,256]{1,0:T(8,128)S(1)}, u32[]{:S(2)}, u32[]{:S(2)}) collective-permute-start(f32[72,256]{1,0:T(8,128)S(1)} %slice_select_fusion.2), channel_id=1, source_target_pairs={{0,16},{1,17},{2,18},{3,19},{4,20},{5,21},{6,22},{7,23},{8,24},{9,... | collective-permute-start | bytes 221192 | tf_op jit(solution)/shard_map/ppermute | solution.py:509
  107.4 3.9 %collective-permute-done.2 = f32[72,256]{1,0:T(8,128)S(1)} collective-permute-done((f32[72,256]{1,0:T(8,128)S(1)}, f32[72,256]{1,0:T(8,128)S(1)}, u32[]{:S(2)}, u32[]{:S(2)}) %collective-permute-start.2) | collective-permute-done | bytes 73760 | tf_op jit(solution)/shard_map/ppermute | solution.py:509
  111.4 2.7 %collective-permute-start.3 = (f32[72,256]{1,0:T(8,128)S(1)}, f32[72,256]{1,0:T(8,128)S(1)}, u32[]{:S(2)}, u32[]{:S(2)}) collective-permute-start(f32[72,256]{1,0:T(8,128)S(1)} %select_add_fusion.2), channel_id=1, source_target_pairs={{0,2},{1,3},{2,0},{3,1},{4,6},{5,7},{6,4},{7,5},{8,10},{9,11},{10,... | collective-permute-start | bytes 221192 | tf_op jit(solution)/shard_map/ppermute | solution.py:509
  114.1 0.1 fusion.targets_in
  114.2 2.5 %collective-permute-done.3 = f32[72,256]{1,0:T(8,128)S(1)} collective-permute-done((f32[72,256]{1,0:T(8,128)S(1)}, f32[72,256]{1,0:T(8,128)S(1)}, u32[]{:S(2)}, u32[]{:S(2)}) %collective-permute-start.3) | collective-permute-done | bytes 73760 | tf_op jit(solution)/shard_map/ppermute | solution.py:509
  116.7 3.0 %collective-permute-start.4 = (f32[72,256]{1,0:T(8,128)S(1)}, f32[72,256]{1,0:T(8,128)S(1)}, u32[]{:S(2)}, u32[]{:S(2)}) collective-permute-start(f32[72,256]{1,0:T(8,128)S(1)} %add.22), channel_id=1, source_target_pairs={{0,4},{1,5},{2,6},{3,7},{4,0},{5,1},{6,2},{7,3},{8,12},{9,13},{10,... | collective-permute-start | bytes 221192 | tf_op jit(solution)/shard_map/ppermute | solution.py:509
  119.7 1.6 %copy-done.8 = bf16[32,128,256]{2,1,0:T(8,128)(2,1)S(1)} copy-done((bf16[32,128,256]{2,1,0:T(8,128)(2,1)S(1)}, bf16[32,128,256]{2,1,0:T(8,128)(2,1)}, u32[]{:S(2)}) %copy-start.8) | copy-done | bytes 2097176
  121.3 3.7 %own_work.1.base_in = f32[4096,256]{1,0:T(8,128)S(1)} custom-call(s32[64]{0:T(128)S(1)} %get-tuple-element.18.by_src, bf16[32,128,128]{2,1,0:T(8,128)(2,1)S(1)} %get-tuple-element.24.own_t, bf16[32,128,256]{2,1,0:T(8,128)(2,1)S(1)} %copy-done.8, bf16[4096,256]{1,0:T(8,128)(2,1)S(1)} %copy-done.7, bf16[256,256]{1,0:T(8,128)(2,1)S(1)} %copy-done.2), custom_call_target="tpu_custom_call" | custom-call | flops 10000000000 | bytes 10485760 | tf_op jit(solution)/shard_map/own_work/pallas_call | solution.py:416
  125.0 1.9 %copy-done.6 = f32[4096,256]{1,0:T(8,128)} copy-done((f32[4096,256]{1,0:T(8,128)}, f32[4096,256]{1,0:T(8,128)S(1)}, u32[]{:S(2)}) %copy-start.6) | copy-done | bytes 4194328
  127.0 3.8 %collective-permute-done.4 = f32[72,256]{1,0:T(8,128)S(1)} collective-permute-done((f32[72,256]{1,0:T(8,128)S(1)}, f32[72,256]{1,0:T(8,128)S(1)}, u32[]{:S(2)}, u32[]{:S(2)}) %collective-permute-start.4) | collective-permute-done | bytes 73760 | tf_op jit(solution)/shard_map/ppermute | solution.py:509
  130.8 0.9 broadcast_in_dim.17
  131.7 3.8 %all-to-all-start.2 = ((f32[8,72,256]{2,1,0:T(8,128)}), f32[8,72,256]{2,1,0:T(8,128)S(1)}, u32[]{:S(2)}, u32[]{:S(2)}) async-start(f32[8,72,256]{2,1,0:T(8,128)} %broadcast_in_dim.17), calls=%async_computation.2 | async-start | bytes 1179648 | tf_op jit(solution)/shard_map/all_to_all | solution.py:505
  135.5 8.9 %scatter_rows.1 = f32[4096,256]{1,0:T(8,128)} custom-call(s32[32,128]{1,0:T(8,128)S(1)} %fusion.targets_in, f32[4096,256]{1,0:T(8,128)} %copy-done.6, bf16[32,128,256]{2,1,0:T(8,128)(2,1)} %all-to-all-done.1.returned_in), custom_call_target="tpu_custom_call" | custom-call | flops 10000000000 | bytes 10485760 | tf_op jit(solution)/shard_map/scatter_rows/pallas_call | solution.py:484
  144.4 0.9 all-to-all-done.2
  145.3 0.6 slice_reduce_fusion
  145.9 0.8 fusion.1
  (28 shorter events, 0.1 us)
Async XLA Ops:
  7.8 7.5 %copy-start.4 = (s32[1,64]{1,0:T(1,128)S(1)}, s32[1,64]{1,0:T(1,128)}, u32[]{:S(2)}) copy-start(s32[1,64]{1,0:T(1,128)} %src.1) | copy-start | bytes 772
  7.8 7.5 %copy-start.5 = (s32[1,64]{1,0:T(1,128)S(1)}, s32[1,64]{1,0:T(1,128)}, u32[]{:S(2)}) copy-start(s32[1,64]{1,0:T(1,128)} %dst.1) | copy-start | bytes 772
  7.8 57.5 %all-to-all-start = ((bf16[32,128,256]{2,1,0:T(8,128)(2,1)}), bf16[32,128,256]{2,1,0:T(8,128)(2,1)}, u32[]{:S(2)}, u32[]{:S(2)}) async-start(bf16[32,128,256]{2,1,0:T(8,128)(2,1)} %gather_rows.1), calls=%async_computation | async-start | bytes 4194304 | tf_op jit(solution)/shard_map/all_to_all | solution.py:505
  15.3 50.0 %copy-start = (bf16[256,256]{1,0:T(8,128)(2,1)S(1)}, bf16[256,256]{1,0:T(8,128)(2,1)}, u32[]{:S(2)}) copy-start(bf16[256,256]{1,0:T(8,128)(2,1)} %w_neigh.3) | copy-start | bytes 393220
  15.3 50.0 %copy-start.1 = (bf16[256,256]{1,0:T(8,128)(2,1)S(1)}, bf16[256,256]{1,0:T(8,128)(2,1)}, u32[]{:S(2)}) copy-start(bf16[256,256]{1,0:T(8,128)(2,1)} %w_self.5) | copy-start | bytes 393220
  15.3 50.0 %copy-start.3 = (f32[256]{0:T(256)S(1)}, f32[256]{0:T(256)}, u32[]{:S(2)}) copy-start(f32[256]{0:T(256)} %param.18) | copy-start | bytes 3076
  21.6 1.3 copy-start.9
  23.0 52.6 %copy-start.10 = (f32[32,8,128]{2,1,0:T(8,128)}, f32[32,8,128]{2,1,0:T(8,128)S(1)}, u32[]{:S(2)}) copy-start(f32[32,8,128]{2,1,0:T(8,128)S(1)} %get-tuple-element.21.scale) | copy-start | bytes 393220
  75.5 55.3 %all-to-all-start.1 = ((bf16[32,128,256]{2,1,0:T(8,128)(2,1)}), bf16[32,128,256]{2,1,0:T(8,128)(2,1)}, u32[]{:S(2)}, u32[]{:S(2)}) async-start(bf16[32,128,256]{2,1,0:T(8,128)(2,1)} %get-tuple-element.28), calls=%async_computation.1 | async-start | bytes 4194304 | tf_op jit(solution)/shard_map/all_to_all | solution.py:505
  88.9 25.2 %copy-start.11 = (s32[1,32,128]{2,1,0:T(8,128)S(1)}, s32[1,32,128]{2,1,0:T(8,128)}, u32[]{:S(2)}) copy-start(s32[1,32,128]{2,1,0:T(8,128)} %param.11) | copy-start | bytes 49156
  88.9 25.1 %copy-start.12 = (s32[1,32]{1,0:T(1,128)S(1)}, s32[1,32]{1,0:T(1,128)}, u32[]{:S(2)}) copy-start(s32[1,32]{1,0:T(1,128)} %counts_in.1) | copy-start | bytes 388
  89.0 30.8 %copy-start.2 = (bf16[256,256]{1,0:T(8,128)(2,1)S(1)}, bf16[256,256]{1,0:T(8,128)(2,1)}, u32[]{:S(2)}) copy-start(bf16[256,256]{1,0:T(8,128)(2,1)} %w_self.5) | copy-start | bytes 393220
  89.0 30.8 %copy-start.7 = (bf16[4096,256]{1,0:T(8,128)(2,1)S(1)}, bf16[4096,256]{1,0:T(8,128)(2,1)}, u32[]{:S(2)}) copy-start(bf16[4096,256]{1,0:T(8,128)(2,1)} %get-tuple-element.26.dpre_b) | copy-start | bytes 6291460
  90.9 1.9 %collective-permute-start = (f32[288,256]{1,0:T(8,128)}, f32[288,256]{1,0:T(8,128)}, u32[]{:S(2)}, u32[]{:S(2)}) collective-permute-start(f32[288,256]{1,0:T(8,128)} %slice_select_fusion), channel_id=1, source_target_pairs={{0,1},{1,0},{2,3},{3,2},{4,5},{5,4},{6,7},{7,6},{8,9},{9,8},{10,11... | collective-permute-start | bytes 884744 | tf_op jit(solution)/shard_map/ppermute | solution.py:509
  96.4 8.2 %collective-permute-start.1 = (f32[144,256]{1,0:T(8,128)}, f32[144,256]{1,0:T(8,128)}, u32[]{:S(2)}, u32[]{:S(2)}) collective-permute-start(f32[144,256]{1,0:T(8,128)} %slice_select_fusion.1), channel_id=1, source_target_pairs={{0,8},{1,9},{2,10},{3,11},{4,12},{5,13},{6,14},{7,15},{8,0},{9,1},... | collective-permute-start | bytes 442376 | tf_op jit(solution)/shard_map/ppermute | solution.py:509
  105.8 5.6 %collective-permute-start.2 = (f32[72,256]{1,0:T(8,128)S(1)}, f32[72,256]{1,0:T(8,128)S(1)}, u32[]{:S(2)}, u32[]{:S(2)}) collective-permute-start(f32[72,256]{1,0:T(8,128)S(1)} %slice_select_fusion.2), channel_id=1, source_target_pairs={{0,16},{1,17},{2,18},{3,19},{4,20},{5,21},{6,22},{7,23},{8,24},{9,... | collective-permute-start | bytes 221192 | tf_op jit(solution)/shard_map/ppermute | solution.py:509
  111.4 5.3 %collective-permute-start.3 = (f32[72,256]{1,0:T(8,128)S(1)}, f32[72,256]{1,0:T(8,128)S(1)}, u32[]{:S(2)}, u32[]{:S(2)}) collective-permute-start(f32[72,256]{1,0:T(8,128)S(1)} %select_add_fusion.2), channel_id=1, source_target_pairs={{0,2},{1,3},{2,0},{3,1},{4,6},{5,7},{6,4},{7,5},{8,10},{9,11},{10,... | collective-permute-start | bytes 221192 | tf_op jit(solution)/shard_map/ppermute | solution.py:509
  116.7 14.1 %collective-permute-start.4 = (f32[72,256]{1,0:T(8,128)S(1)}, f32[72,256]{1,0:T(8,128)S(1)}, u32[]{:S(2)}, u32[]{:S(2)}) collective-permute-start(f32[72,256]{1,0:T(8,128)S(1)} %add.22), channel_id=1, source_target_pairs={{0,4},{1,5},{2,6},{3,7},{4,0},{5,1},{6,2},{7,3},{8,12},{9,13},{10,... | collective-permute-start | bytes 221192 | tf_op jit(solution)/shard_map/ppermute | solution.py:509
  119.7 1.6 %copy-start.8 = (bf16[32,128,256]{2,1,0:T(8,128)(2,1)S(1)}, bf16[32,128,256]{2,1,0:T(8,128)(2,1)}, u32[]{:S(2)}) copy-start(bf16[32,128,256]{2,1,0:T(8,128)(2,1)} %get-tuple-element.25.g) | copy-start | bytes 6291460
  125.0 1.9 %copy-start.6 = (f32[4096,256]{1,0:T(8,128)}, f32[4096,256]{1,0:T(8,128)S(1)}, u32[]{:S(2)}) copy-start(f32[4096,256]{1,0:T(8,128)S(1)} %own_work.1.base_in) | copy-start | bytes 12582916
  131.7 13.6 %all-to-all-start.2 = ((f32[8,72,256]{2,1,0:T(8,128)}), f32[8,72,256]{2,1,0:T(8,128)S(1)}, u32[]{:S(2)}, u32[]{:S(2)}) async-start(f32[8,72,256]{2,1,0:T(8,128)} %broadcast_in_dim.17), calls=%async_computation.2 | async-start | bytes 1179648 | tf_op jit(solution)/shard_map/all_to_all | solution.py:505

commit v3 on v2

--- a/solution.py
+++ b/solution.py
@@ -7,8 +7,10 @@
 from jax.experimental.pallas import tpu as pltpu
 from jax.sharding import PartitionSpec as P
 
+
 AXES = ("row", "col")
 LANES = 128
+MOST_APART = 32
 MIDDLE_MIB = 52
 SCATTER_MIB = 52
 VMEM = pl.BlockSpec(memory_space=pltpu.VMEM)
@@ -51,9 +53,26 @@
     return pl.ds(pl.multiple_of(index * halves, halves), halves)
 
 
-def gather_kernel(picks_in, counts_in, x_in, out_in, picks, counts, x, out, wide, stage, sems):
+def near_peer(me, far_bit, j):
+    low = j & (far_bit - 1)
+    return 2 * (j - low) + low + (me & far_bit)
+
+
+def far_mask(far_bit, j):
+    low = j & (far_bit - 1)
+    return 2 * (j - low) + low + far_bit
+
+
+def my_number(n_col):
+    return lax.axis_index("row") * n_col + lax.axis_index("col")
+
+
+def gather_kernel(whom, n_col, groups, picks_in, counts_in, x_in, *rest):
+    outs, (picks, counts, x, out, wide, stage, sems) = rest[:-7], rest[-7:]
+    me = my_number(n_col)
     rows, width = x.shape
-    peers, slots = picks.shape
+    peers = out.shape[0]
+    slots = picks.shape[1]
     halves = width // LANES
     parts = 4
     chunk = rows // parts
@@ -78,26 +97,44 @@
     copies[0].wait()
     copies[1].wait()
 
-    @pl.loop(0, peers)
-    def _(p):
-        for k in range(slots):
-            stage[row_at(k, halves), :] = wide[row_at(picks[p, k], halves), :]
-        used = lax.broadcasted_iota(jnp.int32, (slots, width), 0) < counts[0, p]
-        out[p] = jnp.where(used, tighten(stage, 0, slots, halves), 0.0).astype(BF16)
-        pltpu.make_async_copy(out.at[p], out_in.at[p], sems.at[2 + parts]).start()
-
-    pltpu.make_async_copy(out, out_in, sems.at[2 + parts]).wait()
-
-
-def gather_rows(x, picks, counts):
+    each = peers // groups
+    for c in range(groups):
+
+        @pl.loop(c * each, (c + 1) * each)
+        def _(j):
+            p = whom(me, j)
+            for k in range(slots):
+                stage[row_at(k, halves), :] = wide[row_at(picks[p, k], halves), :]
+            used = lax.broadcasted_iota(jnp.int32, (slots, width), 0) < counts[0, p]
+            out[j] = jnp.where(used, tighten(stage, 0, slots, halves), 0.0).astype(BF16)
+
+        if len(outs) == 1:
+            at = pl.ds(c * each, each)
+            pltpu.make_async_copy(out.at[at], outs[0].at[at], sems.at[6]).start()
+        else:
+            for j in range(c * each, (c + 1) * each):
+                pltpu.make_async_copy(out.at[j], outs[j // 2].at[j % 2], sems.at[6]).start()
+
+    if len(outs) == 1:
+        pltpu.make_async_copy(out, outs[0], sems.at[6]).wait()
+    else:
+        for j in range(peers):
+            pltpu.make_async_copy(out.at[j], outs[j // 2].at[j % 2], sems.at[6]).wait()
+
+
+def gather_rows(x, picks, counts, whom, n_col, peers, apart):
     rows, width = x.shape
-    peers, slots = picks.shape
+    slots = picks.shape[1]
     halves = width // LANES
+    if apart:
+        out_shape = (jax.ShapeDtypeStruct((2, slots, width), BF16),) * (peers // 2)
+    else:
+        out_shape = (jax.ShapeDtypeStruct((peers, slots, width), BF16),)
     return pl.pallas_call(
-        gather_kernel,
-        out_shape=jax.ShapeDtypeStruct((peers, slots, width), BF16),
+        functools.partial(gather_kernel, whom, n_col, min(4, peers // 2)),
+        out_shape=out_shape,
         in_specs=[ANY, ANY, ANY],
-        out_specs=ANY,
+        out_specs=(ANY,) * len(out_shape),
         scratch_shapes=[
             pltpu.SMEM(picks.shape, jnp.int32),
             pltpu.SMEM(counts.shape, jnp.int32),
@@ -108,14 +145,23 @@
             pltpu.SemaphoreType.DMA((7,)),
         ],
         compiler_params=params(60),
-        cost_estimate=cost(1e10, 4 * rows * width),
+        cost_estimate=cost(1e9, 4 * rows * width),
         name="gather_rows",
     )(picks, counts, x)
 
 
-def local_kernel(src, dst, tiles, adj, edge_t, own_t, by_src, scale, order):
+def peer_at(me, far_bit, peers, i):
+    if not far_bit:
+        return i
+    half = peers // 2
+    far = me ^ far_mask(far_bit, i - half)
+    return jnp.where(i < half, near_peer(me, far_bit, i), far)
+
+
+def local_kernel(n_col, far_bit, src, dst, tiles, adj, edge_t, own_t, by_src, by_turn, scale, order):
     count, tb, _ = tiles.shape
     own = own_t.shape[0]
+    me = my_number(n_col)
 
     @pl.loop(0, count)
     def _(t):
@@ -124,47 +170,44 @@
     scale[...] = jnp.zeros_like(scale)
     ones = jnp.ones((8, tb), BF16)
 
-    def take(s, turned):
+    def take(turn, s):
         t = order[s]
         d = dst[0, t]
         by_src[s] = d
+        by_turn[turn] = d
         tile = tiles[t].astype(F32)
         straight = tile.astype(BF16)
-        adj[s] = straight
-        turned(tile.T.astype(BF16))
+        adj[turn] = straight
         scale[d] += matmul_t(ones, straight)
+        return tile.T.astype(BF16)
 
     @pl.loop(0, own, unroll=4)
     def _(s):
-        def keep(value):
-            own_t[s] = value
-
-        take(s, keep)
-
-    @pl.loop(own, count, unroll=4)
-    def _(s):
-        def keep(value):
-            edge_t[s - own] = value
-
-        take(s, keep)
+        own_t[s] = take(s, s)
+
+    @pl.loop(0, count - own, unroll=4)
+    def _(i):
+        p = peer_at(me, far_bit, count - own, i)
+        edge_t[p] = take(own + i, own + p)
 
     scale[...] = 1.0 / (1.0 + scale[...])
 
 
-def local_work(src, dst, tiles, own):
+def local_work(src, dst, tiles, own, n_col, far_bit):
     count, tb, _ = tiles.shape
     edges = count - own
     return pl.pallas_call(
-        local_kernel,
+        functools.partial(local_kernel, n_col, far_bit),
         out_shape=(
             jax.ShapeDtypeStruct((count, tb, tb), BF16),
             jax.ShapeDtypeStruct((edges, tb, tb), BF16),
             jax.ShapeDtypeStruct((own, tb, tb), BF16),
             jax.ShapeDtypeStruct((count,), jnp.int32),
+            jax.ShapeDtypeStruct((count,), jnp.int32),
             jax.ShapeDtypeStruct((own, 8, tb), F32),
         ),
         in_specs=[SMEM, SMEM, VMEM],
-        out_specs=(VMEM, VMEM, VMEM, SMEM, VMEM),
+        out_specs=(VMEM, VMEM, VMEM, SMEM, SMEM, VMEM),
         scratch_shapes=[pltpu.SMEM((count,), jnp.int32)],
         compiler_params=params(48),
         cost_estimate=cost(2e10, 4 * tiles.size),
@@ -192,11 +235,14 @@
     return pre * sig, dpre
 
 
-def middle_kernel(
-    by_src, arrived, adj, edge_t, x, cot, scale, w_self, w_neigh, bias,
-    agg_out, back_out,
-    arrived_v, adj_v, edge_tv, acc, scale_v, x_v, cot_v, agg_v, g_v, back_v, sems,
-):
+def middle_kernel(far_count, *refs):
+    far, refs = refs[:far_count], refs[far_count:]
+    pairs = far_count // 2
+    (
+        by_src, by_turn, near_in, adj, edge_t, x, cot, scale, w_self, w_neigh, bias,
+        agg_out, back_out,
+        near, adj_v, edge_tv, acc, scale_v, x_v, cot_v, agg_v, g_v, back_v, sems,
+    ) = refs
     own, tb, width = acc.shape
     edges = edge_tv.shape[0]
     rows = own * tb
@@ -214,32 +260,44 @@
     def start_cuts(source, target, size):
         return [start(source.at[at], target.at[at]) for at in cuts(size)]
 
+    near_count = near.shape[0]
+
+    def own_tile(j):
+        return x_v[pl.ds(pl.multiple_of(j * tb, tb), tb), :]
+
+    def fetch_tiles(first, size):
+        at = pl.ds(first, size)
+        return start(adj.at[at], adj_v.at[at])
+
     coming = []
-    for first, size, source, target in ((own, edges, arrived, arrived_v), (0, own, x, x_v)):
-        each = size // parts
-        unit = target.shape[0] // parts
-        for c in range(parts):
-            tiles = pl.ds(first + c * each, each)
-            at = pl.ds(c * unit, unit)
-            needs = start(adj.at[tiles], adj_v.at[tiles]), start(source.at[at], target.at[at])
-            coming.append((first + c * each, each, needs))
+    each = own // parts
+    for c, at in enumerate(cuts(rows)):
+        needs = [fetch_tiles(c * each, each), start(x.at[at], x_v.at[at])]
+        coming.append((own_tile, 0, c * each, each, needs))
+    each = near_count // 2
+    for c in range(2):
+        at = pl.ds(c * each, each)
+        needs = [fetch_tiles(own + c * each, each), start(near_in.at[at], near.at[at])]
+        coming.append((near.__getitem__, own, c * each, each, needs))
+    far_in = [fetch_tiles(own + near_count, far_count)] if far_count else []
     cots = start_cuts(cot, cot_v, rows)
     in_edge_t = start(edge_t, edge_tv)
     acc[...] = jnp.zeros_like(acc)
     spread_scale(scale, scale_v)
 
-    for first, each, needs in coming:
+    for rows_of, base, first, each, needs in coming:
         for copy in needs:
             copy.wait()
 
-        @pl.loop(0, each, unroll=8)
-        def _(i):
-            s = first + i
-            if first < own:
-                block = x_v[pl.ds(pl.multiple_of(s * tb, tb), tb), :]
-            else:
-                block = arrived_v[s - own]
-            acc[by_src[s]] += matmul(adj_v[s], block)
+        @pl.loop(first, first + each, unroll=8)
+        def _(j):
+            acc[by_turn[base + j]] += matmul(adj_v[base + j], rows_of(j))
+
+    for copy in far_in:
+        copy.wait()
+    for i in range(far_count):
+        s = own + near_count + i
+        acc[by_turn[s]] += matmul(adj_v[s], far[i // 2 + (i % 2) * pairs][i % 2])
 
     each = edges // parts
     block = min(8, own // parts)
@@ -277,20 +335,21 @@
         copy.wait()
 
 
-def middle_work(by_src, arrived, adj, edge_t, x, cot, scale, w_self, w_neigh, bias):
-    edges, tb, width = arrived.shape
+def middle_work(far, near, by_src, by_turn, adj, edge_t, x, cot, scale, w_self, w_neigh, bias):
+    edges, tb, _ = edge_t.shape
+    width = x.shape[1]
     own = scale.shape[0]
     rows, hidden = cot.shape
     return pl.pallas_call(
-        middle_kernel,
+        functools.partial(middle_kernel, len(far)),
         out_shape=(
             jax.ShapeDtypeStruct((rows, width), BF16),
             jax.ShapeDtypeStruct((edges, tb, width), BF16),
         ),
-        in_specs=[SMEM] + [ANY] * 5 + [VMEM] * 4,
+        in_specs=[VMEM] * len(far) + [SMEM] * 2 + [ANY] * 5 + [VMEM] * 4,
         out_specs=(ANY, ANY),
         scratch_shapes=[
-            pltpu.VMEM((edges, tb, width), BF16),
+            pltpu.VMEM(near.shape, BF16),
             pltpu.VMEM((own + edges, tb, tb), BF16),
             pltpu.VMEM((edges, tb, tb), BF16),
             pltpu.VMEM((own, tb, width), F32),
@@ -300,12 +359,12 @@
             pltpu.VMEM((rows, width), BF16),
             pltpu.VMEM((own, tb, width), BF16),
             pltpu.VMEM((edges, tb, width), BF16),
-            pltpu.SemaphoreType.DMA((32,)),
+            pltpu.SemaphoreType.DMA((80,)),
         ],
         compiler_params=params(MIDDLE_MIB),
         cost_estimate=cost(2e10, 16 * rows * width),
         name="middle_work",
-    )(by_src, arrived, adj, edge_t, x, cot, scale, w_self, w_neigh, bias)
+    )(*far, by_src, by_turn, near, adj, edge_t, x, cot, scale, w_self, w_neigh, bias)
 
 
 def tail_kernel(
@@ -313,7 +372,7 @@
     layer_out, dpre_out, g_out, terms,
     agg, x, cot, layer_v, dpre_v, g_v, scale_v, sems,
 ):
-    rows, width = x.shape
+    _, width = x.shape
     own, tb, _ = g_v.shape
     hidden = cot.shape[1]
     block = 4
@@ -402,7 +461,7 @@
 
 
 def own_kernel(by_src, own_t, g, dpre_b, w_self, out):
-    own, tb, width = g.shape
+    own, tb, _ = g.shape
 
     @pl.loop(0, own, unroll=4)
     def _(s):
@@ -505,6 +564,46 @@
     return lax.all_to_all(block, AXES, 0, 0, tiled=True, axis_index_groups=groups)
 
 
+def fetch_rows(features, picks, counts, shape):
+    n_row, n_col = shape
+    members = n_row * n_col
+    far_bit = n_col // 2
+    if members > MOST_APART:
+        (outgoing,) = gather_rows(
+            features, picks, counts, lambda me, j: j, n_col, members, False
+        )
+        return (), exchange(outgoing)
+    half = members // 2
+    pairs = half // 2
+    soon = pairs // 4
+
+    def gather_far(first, count):
+        def whom(me, j):
+            return me ^ far_mask(far_bit, 2 * first + j)
+
+        return gather_rows(features, picks, counts, whom, n_col, 2 * count, True)
+
+    def cross(blocks, first):
+        return tuple(
+            flip(block, far_mask(far_bit, 2 * (first + j)), members)
+            for j, block in enumerate(blocks)
+        )
+
+    first_blocks = gather_far(0, soon)
+    crossed = cross(first_blocks, 0)
+    features, _ = lax.optimization_barrier((features, first_blocks[0]))
+    outgoing = gather_far(soon, pairs - soon)
+    crossed += cross(outgoing[: pairs // 2 - soon], soon)
+    crossed += cross(outgoing[pairs // 2 - soon :], pairs // 2)
+    features, _ = lax.optimization_barrier((features, outgoing[0]))
+    far = crossed + tuple(flip(block, 1, members) for block in crossed)
+    (outgoing,) = gather_rows(
+        features, picks, counts, lambda me, j: near_peer(me, far_bit, j), n_col, half, False
+    )
+    groups = [[near_peer(side, far_bit, j) for j in range(half)] for side in (0, far_bit)]
+    return far, exchange(outgoing, groups)
+
+
 def flip(value, bit, members):
     return lax.ppermute(value, AXES, [(i, i ^ bit) for i in range(members)])
 
@@ -550,15 +649,27 @@
     shape, features, send_rows, counts, tile_dst, tile_src, tiles, w_self, w_neigh, bias, cotangent
 ):
     rows, width = features.shape
-    peers, slots = send_rows.shape[1:]
+    _, slots = send_rows.shape[1:]
     picks = send_rows[0]
-    outgoing = gather_rows(features, picks, counts)
-    arrived = exchange(outgoing)
-    adj, edge_t, own_t, by_src, scale = local_work(tile_src, tile_dst, tiles[0], rows // slots)
+    far, near = fetch_rows(features, picks, counts, shape)
+    adj, edge_t, own_t, by_src, by_turn, scale = local_work(
+        tile_src, tile_dst, tiles[0], rows // slots, shape[1], shape[1] // 2 if far else 0
+    )
     keep = jnp.arange(slots, dtype=jnp.int32)[None, :] < counts[0][:, None]
     targets = jnp.where(keep, picks, rows)
     agg, back_b = middle_work(
-        by_src, arrived, adj, edge_t, features, cotangent, scale, w_self, w_neigh, bias[None]
+        far,
+        near,
+        by_src,
+        by_turn,
+        adj,
+        edge_t,
+        features,
+        cotangent,
+        scale,
+        w_self,
+        w_neigh,
+        bias[None],
     )
     returned = exchange(back_b)
     spare = 8 << len(split_bits(shape)[0])

time: 147 us -> 159 us (1.082)
  starting transfers between devices: 23.7 us -> 49.9 us
  waiting for transfers between devices: 62.2 us -> 40.6 us
  Pallas kernels: 46 us -> 51.7 us
  local copies, waits for them, and re-layouts: 6.59 us -> 8.23 us
    all_to_all x3, waiting for transfers between devices: 43.2 us -> 6.12 us  [exchange(): lax.all_to_all(block, AXES, 0, 0, tiled=True, axis_index_groups=groups)]
    ppermute x5 -> x21, starting transfers between devices: 8.81 us -> 38.1 us  [flip(): return lax.ppermute(value, AXES, [(i, i ^ bit) for i in range(members)])]
    ppermute x5 -> x21, waiting for transfers between devices: 19 us -> 34.4 us  [flip(): return lax.ppermute(value, AXES, [(i, i ^ bit) for i in range(members)])]
    pallas_call x3 -> x5, Pallas kernels: 23.7 us -> 29.4 us  [the longest x3 12 us: gather_rows(): pl.pallas_call(functools.partial(gather_kernel, whom, n_col, min(4, peers...]
    all_to_all x3, starting transfers between devices: 14.9 us -> 11.8 us  [exchange(): lax.all_to_all(block, AXES, 0, 0, tiled=True, axis_index_groups=groups)]
    unnamed x26, local copies, waits for them, and re-layouts: 4.9 us -> 6.55 us
  transfers between devices with their start and end apart: 8 -> 24, of which waited for: 7 -> 9; matrix products, arithmetic and copies ran while one was open for 5% -> 4% of each run, Pallas kernels for 20% -> 24%
where the time goes in v3:
time: 159 us; the launch traced here: 158 us
  Pallas kernels  51.7 us (33%)
  starting transfers between devices  49.9 us (31%)
  waiting for transfers between devices  40.6 us (26%)
  local copies, waits for them, and re-layouts  8.23 us (5%)
  other arithmetic  7.24 us (5%)
    ppermute x21, starting transfers between devices, flip(): return lax.ppermute(value, AXES, [(i, i ^ bit) for i in range(members)])  38.1 us
    ppermute x21, waiting for transfers between devices, flip(): return lax.ppermute(value, AXES, [(i, i ^ bit) for i in range(members)])  34.4 us
    pallas_call x3, Pallas kernels, gather_rows(): pl.pallas_call(functools.partial(gather_kernel, whom, n_col, min(4, peers...  12 us
    all_to_all x3, starting transfers between devices, exchange(): lax.all_to_all(block, AXES, 0, 0, tiled=True, axis_index_groups=groups)  11.8 us
    pallas_call x1, Pallas kernels, middle_work(): pl.pallas_call(functools.partial(middle_kernel, len(far)), out_shape=(jax...  11 us
    pallas_call x1, Pallas kernels, tail_work(): pl.pallas_call(tail_kernel, out_shape=(jax.ShapeDtypeStruct((rows, hidden...  9.66 us
    pallas_call x1, Pallas kernels, scatter_rows(): pl.pallas_call(scatter_kernel, out_shape=jax.ShapeDtypeStruct((rows, widt...  8.91 us
    unnamed x26, local copies, waits for them, and re-layouts  6.55 us
  transfers between devices with their start and end apart: 24, of which 9 were waited for; matrix products, arithmetic and copies ran while one was open for 4% of the time, Pallas kernels for 24%

profile of v3, /device:TPU:0, one launch (start us, length us, event | category | flops | bytes accessed | tf_op | source)
XLA Modules:
  0.0 158.4 jit_solution(2071954524715435909)
XLA Ops:
  0.6 3.0 %gather_rows.3 = (bf16[2,128,256]{2,1,0:T(8,128)(2,1)}, bf16[2,128,256]{2,1,0:T(8,128)(2,1)}) custom-call(s32[32,128]{1,0:T(8,128)} %bitcast.10, s32[1,32]{1,0:T(1,128)} %counts_in.5, bf16[4096,256]{1,0:T(8,128)(2,1)} %x_in.5), custom_call_target="tpu_custom_call" | custom-call | flops 1000000000 | bytes 4194304 | tf_op jit(solution)/shard_map/gather_rows/pallas_call | solution.py:133
  3.6 5.1 %collective-permute-start.1 = (bf16[2,128,256]{2,1,0:T(8,128)(2,1)}, bf16[2,128,256]{2,1,0:T(8,128)(2,1)S(1)}, u32[]{:S(2)}, u32[]{:S(2)}) collective-permute-start(bf16[2,128,256]{2,1,0:T(8,128)(2,1)} %get-tuple-element.30), channel_id=1, source_target_pairs={{0,6},{1,7},{2,4},{3,5},{4,2},{5,3},{6,0},{7,1},{8,14},{9,15},{10,... | collective-permute-start | bytes 393224 | tf_op jit(solution)/shard_map/ppermute | solution.py:608
  8.7 4.2 %gather_rows.4 = (bf16[2,128,256]{2,1,0:T(8,128)(2,1)}, bf16[2,128,256]{2,1,0:T(8,128)(2,1)}, bf16[2,128,256]{2,1,0:T(8,128)(2,1)}, bf16[2,128,256]{2,1,0:T(8,12...) custom-call(s32[32,128]{1,0:T(8,128)} %bitcast.11, s32[1,32]{1,0:T(1,128)} %counts_in.5, ...), custom_call_target="tpu_custom_call" | custom-call | flops 1000000000 | bytes 4194304 | tf_op jit(solution)/shard_map/gather_rows/pallas_call | solution.py:133
  13.0 2.9 %collective-permute-start.3 = (bf16[2,128,256]{2,1,0:T(8,128)(2,1)}, bf16[2,128,256]{2,1,0:T(8,128)(2,1)S(1)}, u32[]{:S(2)}, u32[]{:S(2)}) collective-permute-start(bf16[2,128,256]{2,1,0:T(8,128)(2,1)} %get-tuple-element.33), channel_id=1, source_target_pairs={{0,14},{1,15},{2,12},{3,13},{4,10},{5,11},{6,8},{7,9},{8,6},{9,7},... | collective-permute-start | bytes 393224 | tf_op jit(solution)/shard_map/ppermute | solution.py:608
  17.2 3.5 %collective-permute-start.5 = (bf16[2,128,256]{2,1,0:T(8,128)(2,1)}, bf16[2,128,256]{2,1,0:T(8,128)(2,1)S(1)}, u32[]{:S(2)}, u32[]{:S(2)}) collective-permute-start(bf16[2,128,256]{2,1,0:T(8,128)(2,1)} %get-tuple-element.35), channel_id=1, source_target_pairs={{0,22},{1,23},{2,20},{3,21},{4,18},{5,19},{6,16},{7,17},{8,30},{9,... | collective-permute-start | bytes 393224 | tf_op jit(solution)/shard_map/ppermute | solution.py:608
  20.7 10.9 %collective-permute-start.6 = (bf16[2,128,256]{2,1,0:T(8,128)(2,1)}, bf16[2,128,256]{2,1,0:T(8,128)(2,1)S(1)}, u32[]{:S(2)}, u32[]{:S(2)}) collective-permute-start(bf16[2,128,256]{2,1,0:T(8,128)(2,1)} %get-tuple-element.36), channel_id=1, source_target_pairs={{0,28},{1,29},{2,30},{3,31},{4,24},{5,25},{6,26},{7,27},{8,20},{9,... | collective-permute-start | bytes 393224 | tf_op jit(solution)/shard_map/ppermute | solution.py:608
  31.7 3.8 %collective-permute-start.7 = (bf16[2,128,256]{2,1,0:T(8,128)(2,1)}, bf16[2,128,256]{2,1,0:T(8,128)(2,1)S(1)}, u32[]{:S(2)}, u32[]{:S(2)}) collective-permute-start(bf16[2,128,256]{2,1,0:T(8,128)(2,1)} %get-tuple-element.37), channel_id=1, source_target_pairs={{0,30},{1,31},{2,28},{3,29},{4,26},{5,27},{6,24},{7,25},{8,22},{9,... | collective-permute-start | bytes 393224 | tf_op jit(solution)/shard_map/ppermute | solution.py:608
  35.4 9.0 %collective-permute-done.4.refs_4_ = bf16[2,128,256]{2,1,0:T(8,128)(2,1)S(1)} collective-permute-done((bf16[2,128,256]{2,1,0:T(8,128)(2,1)}, bf16[2,128,256]{2,1,0:T(8,128)(2,1)S(1)}, u32[]{:S(2)}, u32[]{:S(2)}) %collective-permute-start.4) | collective-permute-done | bytes 131104 | tf_op jit(solution)/shard_map/ppermute | solution.py:608
  44.9 6.0 %collective-permute-done.6.refs_6_ = bf16[2,128,256]{2,1,0:T(8,128)(2,1)S(1)} collective-permute-done((bf16[2,128,256]{2,1,0:T(8,128)(2,1)}, bf16[2,128,256]{2,1,0:T(8,128)(2,1)S(1)}, u32[]{:S(2)}, u32[]{:S(2)}) %collective-permute-start.6) | collective-permute-done | bytes 131104 | tf_op jit(solution)/shard_map/ppermute | solution.py:608
  51.0 4.8 %gather_rows.5 = bf16[16,128,256]{2,1,0:T(8,128)(2,1)} custom-call(s32[32,128]{1,0:T(8,128)} %bitcast.12, s32[1,32]{1,0:T(1,128)} %counts_in.5, bf16[4096,256]{1,0:T(8,128)(2,1)} %x_in.5), custom_call_target="tpu_custom_call" | custom-call | flops 1000000000 | bytes 4194304 | tf_op jit(solution)/shard_map/gather_rows/pallas_call | solution.py:133
  55.8 4.3 %all-to-all-start = ((bf16[16,128,256]{2,1,0:T(8,128)(2,1)}), bf16[16,128,256]{2,1,0:T(8,128)(2,1)}, u32[]{:S(2)}, u32[]{:S(2)}) async-start(bf16[16,128,256]{2,1,0:T(8,128)(2,1)} %gather_rows.5), calls=%async_computation | async-start | bytes 2097152 | tf_op jit(solution)/shard_map/all_to_all | solution.py:564
  61.7 6.4 %local_work.1 = (bf16[64,128,128]{2,1,0:T(8,128)(2,1)S(1)}, bf16[32,128,128]{2,1,0:T(8,128)(2,1)S(1)}, bf16[32,128,128]{2,1,0:T(8,128)(2,1)S(1)}, s32[64]{0:T(12...) custom-call(s32[1,64]{1,0:T(1,128)S(1)} %copy-done.2, s32[1,64]{1,0:T(1,128)S(1)} %copy-done.3, s32[64,128,128]{2,1,0:T(8,128)} %bitcast.14), custom_call_target="tpu_custom_call" | custom-call | flops 20000000000 | bytes 4194304 | tf_op jit(solution)/shard_map/local_work/pallas_call | solution.py:199
  71.1 5.2 %all-to-all-done.refs_18_ = bf16[16,128,256]{2,1,0:T(8,128)(2,1)} async-done(((bf16[16,128,256]{2,1,0:T(8,128)(2,1)}), bf16[16,128,256]{2,1,0:T(8,128)(2,1)}, u32[]{:S(2)}, u32[]{:S(2)}) %all-to-all-start) | async-done | bytes 1048608 | tf_op jit(solution)/shard_map/all_to_all | solution.py:564
  76.3 11.0 %middle_work.1 = (bf16[4096,256]{1,0:T(8,128)(2,1)}, bf16[32,128,256]{2,1,0:T(8,128)(2,1)}) custom-call(bf16[2,128,256]{2,1,0:T(8,128)(2,1)S(1)} %collective-permute-done.refs_0_, bf16[2,128,256]{2,1,0:T(8,128)(2,1)S(1)} %collective-permute-done.1.refs_1_, bf16[2,128,256]{2,1,0:T(8,128)(2,1)S(1)} %collective-permute-done.2.refs_2_, ...), custom_call_target="tpu_custom_call" | custom-call | flops 20000000000 | bytes 16777216 | tf_op jit(solution)/shard_map/middle_work/pallas_call | solution.py:343
  87.3 3.7 %all-to-all-start.1 = ((bf16[32,128,256]{2,1,0:T(8,128)(2,1)}), bf16[32,128,256]{2,1,0:T(8,128)(2,1)}, u32[]{:S(2)}, u32[]{:S(2)}) async-start(bf16[32,128,256]{2,1,0:T(8,128)(2,1)} %get-tuple-element.50), calls=%async_computation.1 | async-start | bytes 4194304 | tf_op jit(solution)/shard_map/all_to_all | solution.py:564
  91.0 9.7 %tail_work.1 = (bf16[4096,256]{1,0:T(8,128)(2,1)}, bf16[4096,256]{1,0:T(8,128)(2,1)}, bf16[32,128,256]{2,1,0:T(8,128)(2,1)}, f32[576,256]{1,0:T(8,128)}) custom-call(bf16[4096,256]{1,0:T(8,128)(2,1)} %get-tuple-element.44.agg_in, bf16[4096,256]{1,0:T(8,128)(2,1)} %x_in.5, bf16[4096,256]{1,0:T(8,128)(2,1)} %cot_in.1, f32[32,8,128]{2,1,0:T(8,128)} %copy-done.9, ...), custom_call_target="tpu_custom_call" | custom-call | flops 10000000000 | bytes 16777216 | tf_op jit(solution)/shard_map/tail_work/pallas_call | solution.py:437
  100.7 2.0 %slice_select_fusion = f32[288,256]{1,0:T(8,128)} fusion(f32[576,256]{1,0:T(8,128)} %get-tuple-element.49, pred[]{:T(512)S(6)} %ne.11), kind=kLoop, calls=%fused_computation.1 | loop fusion | flops 73728 | bytes 884737 | tf_op jit(solution)/shard_map/jit(_where)/select_n | solution.py:627
  102.7 1.9 %collective-permute-done.16 = f32[288,256]{1,0:T(8,128)} collective-permute-done((f32[288,256]{1,0:T(8,128)}, f32[288,256]{1,0:T(8,128)}, u32[]{:S(2)}, u32[]{:S(2)}) %collective-permute-start.16) | collective-permute-done | bytes 294944 | tf_op jit(solution)/shard_map/ppermute | solution.py:608
  104.6 1.9 %select_add_fusion = f32[288,256]{1,0:T(8,128)} fusion(f32[288,256]{1,0:T(8,128)} %collective-permute-done.16, f32[576,256]{1,0:T(8,128)} %get-tuple-element.49, pred[]{:T(512)S(6)} %ne.11), kind=kLoop, calls=%fused_computation | loop fusion | flops 147456 | bytes 1179649 | tf_op jit(solution)/shard_map/add | solution.py:627
  106.5 1.7 %slice_select_fusion.1 = f32[144,256]{1,0:T(8,128)} fusion(f32[288,256]{1,0:T(8,128)} %select_add_fusion, pred[]{:T(512)S(6)} %ne.10), kind=kLoop, calls=%fused_computation.3 | loop fusion | flops 36864 | bytes 442369 | tf_op jit(solution)/shard_map/jit(_where)/select_n | solution.py:627
  109.5 6.8 %collective-permute-done.17 = f32[144,256]{1,0:T(8,128)S(1)} collective-permute-done((f32[144,256]{1,0:T(8,128)}, f32[144,256]{1,0:T(8,128)S(1)}, u32[]{:S(2)}, u32[]{:S(2)}) %collective-permute-start.17) | collective-permute-done | bytes 147488 | tf_op jit(solution)/shard_map/ppermute | solution.py:608
  117.3 1.6 %collective-permute-start.18 = (f32[72,256]{1,0:T(8,128)S(1)}, f32[72,256]{1,0:T(8,128)S(1)}, u32[]{:S(2)}, u32[]{:S(2)}) collective-permute-start(f32[72,256]{1,0:T(8,128)S(1)} %slice_select_fusion.2), channel_id=1, source_target_pairs={{0,16},{1,17},{2,18},{3,19},{4,20},{5,21},{6,22},{7,23},{8,24},{9,... | collective-permute-start | bytes 221192 | tf_op jit(solution)/shard_map/ppermute | solution.py:608
  119.0 4.1 %collective-permute-done.18 = f32[72,256]{1,0:T(8,128)S(1)} collective-permute-done((f32[72,256]{1,0:T(8,128)S(1)}, f32[72,256]{1,0:T(8,128)S(1)}, u32[]{:S(2)}, u32[]{:S(2)}) %collective-permute-start.18) | collective-permute-done | bytes 73760 | tf_op jit(solution)/shard_map/ppermute | solution.py:608
  123.1 2.5 %collective-permute-start.19 = (f32[72,256]{1,0:T(8,128)S(1)}, f32[72,256]{1,0:T(8,128)S(1)}, u32[]{:S(2)}, u32[]{:S(2)}) collective-permute-start(f32[72,256]{1,0:T(8,128)S(1)} %select_add_fusion.2), channel_id=1, source_target_pairs={{0,2},{1,3},{2,0},{3,1},{4,6},{5,7},{6,4},{7,5},{8,10},{9,11},{10,... | collective-permute-start | bytes 221192 | tf_op jit(solution)/shard_map/ppermute | solution.py:608
  125.7 2.8 %collective-permute-done.19 = f32[72,256]{1,0:T(8,128)S(1)} collective-permute-done((f32[72,256]{1,0:T(8,128)S(1)}, f32[72,256]{1,0:T(8,128)S(1)}, u32[]{:S(2)}, u32[]{:S(2)}) %collective-permute-start.19) | collective-permute-done | bytes 73760 | tf_op jit(solution)/shard_map/ppermute | solution.py:608
  128.5 3.0 %collective-permute-start.20 = (f32[72,256]{1,0:T(8,128)S(1)}, f32[72,256]{1,0:T(8,128)S(1)}, u32[]{:S(2)}, u32[]{:S(2)}) collective-permute-start(f32[72,256]{1,0:T(8,128)S(1)} %add.22), channel_id=1, source_target_pairs={{0,4},{1,5},{2,6},{3,7},{4,0},{5,1},{6,2},{7,3},{8,12},{9,13},{10,... | collective-permute-start | bytes 221192 | tf_op jit(solution)/shard_map/ppermute | solution.py:608
  131.5 1.6 %copy-done.6 = bf16[32,128,256]{2,1,0:T(8,128)(2,1)S(1)} copy-done((bf16[32,128,256]{2,1,0:T(8,128)(2,1)S(1)}, bf16[32,128,256]{2,1,0:T(8,128)(2,1)}, u32[]{:S(2)}) %copy-start.6) | copy-done | bytes 2097176
  133.1 3.7 %own_work.1.base_in = f32[4096,256]{1,0:T(8,128)S(1)} custom-call(s32[64]{0:T(128)S(1)} %get-tuple-element.38.refs_16_.by_src, bf16[32,128,128]{2,1,0:T(8,128)(2,1)S(1)} %get-tuple-element.46.own_t, bf16[32,128,256]{2,1,0:T(8,128)(2,1)S(1)} %copy-done.6, bf16[4096,256]{1,0:T(8,128)(2,1)S(1)} %copy-done.5, bf16[256,256]{1,0:T(8,128)(2,1)S(1)} %copy-done), custom_call_target="tpu_custom_call" | custom-call | flops 10000000000 | bytes 10485760 | tf_op jit(solution)/shard_map/own_work/pallas_call | solution.py:475
  136.8 2.0 %copy-done.4 = f32[4096,256]{1,0:T(8,128)} copy-done((f32[4096,256]{1,0:T(8,128)}, f32[4096,256]{1,0:T(8,128)S(1)}, u32[]{:S(2)}) %copy-start.4) | copy-done | bytes 4194328
  138.8 3.8 %collective-permute-done.20 = f32[72,256]{1,0:T(8,128)S(1)} collective-permute-done((f32[72,256]{1,0:T(8,128)S(1)}, f32[72,256]{1,0:T(8,128)S(1)}, u32[]{:S(2)}, u32[]{:S(2)}) %collective-permute-start.20) | collective-permute-done | bytes 73760 | tf_op jit(solution)/shard_map/ppermute | solution.py:608
  143.4 3.8 %all-to-all-start.2 = ((f32[8,72,256]{2,1,0:T(8,128)}), f32[8,72,256]{2,1,0:T(8,128)S(1)}, u32[]{:S(2)}, u32[]{:S(2)}) async-start(f32[8,72,256]{2,1,0:T(8,128)} %broadcast_in_dim.17), calls=%async_computation.2 | async-start | bytes 1179648 | tf_op jit(solution)/shard_map/all_to_all | solution.py:564
  147.2 8.9 %scatter_rows.1 = f32[4096,256]{1,0:T(8,128)} custom-call(s32[32,128]{1,0:T(8,128)S(1)} %fusion.targets_in, f32[4096,256]{1,0:T(8,128)} %copy-done.4, bf16[32,128,256]{2,1,0:T(8,128)(2,1)} %all-to-all-done.1.returned_in), custom_call_target="tpu_custom_call" | custom-call | flops 10000000000 | bytes 10485760 | tf_op jit(solution)/shard_map/scatter_rows/pallas_call | solution.py:543
  (62 shorter events, 12.0 us)
Async XLA Ops:
  3.6 17.1 %collective-permute-start.1 = (bf16[2,128,256]{2,1,0:T(8,128)(2,1)}, bf16[2,128,256]{2,1,0:T(8,128)(2,1)S(1)}, u32[]{:S(2)}, u32[]{:S(2)}) collective-permute-start(bf16[2,128,256]{2,1,0:T(8,128)(2,1)} %get-tuple-element.30), channel_id=1, source_target_pairs={{0,6},{1,7},{2,4},{3,5},{4,2},{5,3},{6,0},{7,1},{8,14},{9,15},{10,... | collective-permute-start | bytes 393224 | tf_op jit(solution)/shard_map/ppermute | solution.py:608
  8.7 22.9 %collective-permute-start = (bf16[2,128,256]{2,1,0:T(8,128)(2,1)}, bf16[2,128,256]{2,1,0:T(8,128)(2,1)S(1)}, u32[]{:S(2)}, u32[]{:S(2)}) collective-permute-start(bf16[2,128,256]{2,1,0:T(8,128)(2,1)} %get-tuple-element.29), channel_id=1, source_target_pairs={{0,4},{1,5},{2,6},{3,7},{4,0},{5,1},{6,2},{7,3},{8,12},{9,13},{10,... | collective-permute-start | bytes 393224 | tf_op jit(solution)/shard_map/ppermute | solution.py:608
  13.0 18.7 %collective-permute-start.3 = (bf16[2,128,256]{2,1,0:T(8,128)(2,1)}, bf16[2,128,256]{2,1,0:T(8,128)(2,1)S(1)}, u32[]{:S(2)}, u32[]{:S(2)}) collective-permute-start(bf16[2,128,256]{2,1,0:T(8,128)(2,1)} %get-tuple-element.33), channel_id=1, source_target_pairs={{0,14},{1,15},{2,12},{3,13},{4,10},{5,11},{6,8},{7,9},{8,6},{9,7},... | collective-permute-start | bytes 393224 | tf_op jit(solution)/shard_map/ppermute | solution.py:608
  15.9 28.5 %collective-permute-start.4 = (bf16[2,128,256]{2,1,0:T(8,128)(2,1)}, bf16[2,128,256]{2,1,0:T(8,128)(2,1)S(1)}, u32[]{:S(2)}, u32[]{:S(2)}) collective-permute-start(bf16[2,128,256]{2,1,0:T(8,128)(2,1)} %get-tuple-element.34), channel_id=1, source_target_pairs={{0,20},{1,21},{2,22},{3,23},{4,16},{5,17},{6,18},{7,19},{8,28},{9,... | collective-permute-start | bytes 393224 | tf_op jit(solution)/shard_map/ppermute | solution.py:608
  17.2 27.3 %collective-permute-start.5 = (bf16[2,128,256]{2,1,0:T(8,128)(2,1)}, bf16[2,128,256]{2,1,0:T(8,128)(2,1)S(1)}, u32[]{:S(2)}, u32[]{:S(2)}) collective-permute-start(bf16[2,128,256]{2,1,0:T(8,128)(2,1)} %get-tuple-element.35), channel_id=1, source_target_pairs={{0,22},{1,23},{2,20},{3,21},{4,18},{5,19},{6,16},{7,17},{8,30},{9,... | collective-permute-start | bytes 393224 | tf_op jit(solution)/shard_map/ppermute | solution.py:608
  20.7 30.2 %collective-permute-start.6 = (bf16[2,128,256]{2,1,0:T(8,128)(2,1)}, bf16[2,128,256]{2,1,0:T(8,128)(2,1)S(1)}, u32[]{:S(2)}, u32[]{:S(2)}) collective-permute-start(bf16[2,128,256]{2,1,0:T(8,128)(2,1)} %get-tuple-element.36), channel_id=1, source_target_pairs={{0,28},{1,29},{2,30},{3,31},{4,24},{5,25},{6,26},{7,27},{8,20},{9,... | collective-permute-start | bytes 393224 | tf_op jit(solution)/shard_map/ppermute | solution.py:608
  31.6 29.0 %collective-permute-start.2 = (bf16[2,128,256]{2,1,0:T(8,128)(2,1)}, bf16[2,128,256]{2,1,0:T(8,128)(2,1)S(1)}, u32[]{:S(2)}, u32[]{:S(2)}) collective-permute-start(bf16[2,128,256]{2,1,0:T(8,128)(2,1)} %get-tuple-element.32), channel_id=1, source_target_pairs={{0,12},{1,13},{2,14},{3,15},{4,8},{5,9},{6,10},{7,11},{8,4},{9,5},... | collective-permute-start | bytes 393224 | tf_op jit(solution)/shard_map/ppermute | solution.py:608
  31.7 30.0 %copy-start.2 = (s32[1,64]{1,0:T(1,128)S(1)}, s32[1,64]{1,0:T(1,128)}, u32[]{:S(2)}) copy-start(s32[1,64]{1,0:T(1,128)} %src.1) | copy-start | bytes 772
  31.7 30.0 %copy-start.3 = (s32[1,64]{1,0:T(1,128)S(1)}, s32[1,64]{1,0:T(1,128)}, u32[]{:S(2)}) copy-start(s32[1,64]{1,0:T(1,128)} %dst.1) | copy-start | bytes 772
  31.7 28.5 %collective-permute-start.7 = (bf16[2,128,256]{2,1,0:T(8,128)(2,1)}, bf16[2,128,256]{2,1,0:T(8,128)(2,1)S(1)}, u32[]{:S(2)}, u32[]{:S(2)}) collective-permute-start(bf16[2,128,256]{2,1,0:T(8,128)(2,1)} %get-tuple-element.37), channel_id=1, source_target_pairs={{0,30},{1,31},{2,28},{3,29},{4,26},{5,27},{6,24},{7,25},{8,22},{9,... | collective-permute-start | bytes 393224 | tf_op jit(solution)/shard_map/ppermute | solution.py:608
  44.4 16.3 %collective-permute-start.9 = (bf16[2,128,256]{2,1,0:T(8,128)(2,1)S(1)}, bf16[2,128,256]{2,1,0:T(8,128)(2,1)S(1)}, u32[]{:S(2)}, u32[]{:S(2)}) collective-permute-start(bf16[2,128,256]{2,1,0:T(8,128)(2,1)S(1)} %collective-permute-done.1.refs_1_), channel_id=1, source_target_pairs={{0,1},{1,0},{2,3},{3,2},{4,5},{5,4},{6,7},{7,6},{8,9},{9,8},{10,11... | collective-permute-start | bytes 393224 | tf_op jit(solution)/shard_map/ppermute | solution.py:608
  44.4 16.7 %collective-permute-start.8 = (bf16[2,128,256]{2,1,0:T(8,128)(2,1)S(1)}, bf16[2,128,256]{2,1,0:T(8,128)(2,1)S(1)}, u32[]{:S(2)}, u32[]{:S(2)}) collective-permute-start(bf16[2,128,256]{2,1,0:T(8,128)(2,1)S(1)} %collective-permute-done.refs_0_), channel_id=1, source_target_pairs={{0,1},{1,0},{2,3},{3,2},{4,5},{5,4},{6,7},{7,6},{8,9},{9,8},{10,11... | collective-permute-start | bytes 393224 | tf_op jit(solution)/shard_map/ppermute | solution.py:608
  50.9 10.3 %collective-permute-start.11 = (bf16[2,128,256]{2,1,0:T(8,128)(2,1)S(1)}, bf16[2,128,256]{2,1,0:T(8,128)(2,1)S(1)}, u32[]{:S(2)}, u32[]{:S(2)}) collective-permute-start(bf16[2,128,256]{2,1,0:T(8,128)(2,1)S(1)} %collective-permute-done.3.refs_3_), channel_id=1, source_target_pairs={{0,1},{1,0},{2,3},{3,2},{4,5},{5,4},{6,7},{7,6},{8,9},{9,8},{10,11... | collective-permute-start | bytes 393224 | tf_op jit(solution)/shard_map/ppermute | solution.py:608
  55.8 20.5 %all-to-all-start = ((bf16[16,128,256]{2,1,0:T(8,128)(2,1)}), bf16[16,128,256]{2,1,0:T(8,128)(2,1)}, u32[]{:S(2)}, u32[]{:S(2)}) async-start(bf16[16,128,256]{2,1,0:T(8,128)(2,1)} %gather_rows.5), calls=%async_computation | async-start | bytes 2097152 | tf_op jit(solution)/shard_map/all_to_all | solution.py:564
  60.2 10.9 %collective-permute-start.12 = (bf16[2,128,256]{2,1,0:T(8,128)(2,1)S(1)}, bf16[2,128,256]{2,1,0:T(8,128)(2,1)S(1)}, u32[]{:S(2)}, u32[]{:S(2)}) collective-permute-start(bf16[2,128,256]{2,1,0:T(8,128)(2,1)S(1)} %collective-permute-done.4.refs_4_), channel_id=1, source_target_pairs={{0,1},{1,0},{2,3},{3,2},{4,5},{5,4},{6,7},{7,6},{8,9},{9,8},{10,11... | collective-permute-start | bytes 393224 | tf_op jit(solution)/shard_map/ppermute | solution.py:608
  60.6 10.4 %collective-permute-start.13 = (bf16[2,128,256]{2,1,0:T(8,128)(2,1)S(1)}, bf16[2,128,256]{2,1,0:T(8,128)(2,1)S(1)}, u32[]{:S(2)}, u32[]{:S(2)}) collective-permute-start(bf16[2,128,256]{2,1,0:T(8,128)(2,1)S(1)} %collective-permute-done.5.refs_5_), channel_id=1, source_target_pairs={{0,1},{1,0},{2,3},{3,2},{4,5},{5,4},{6,7},{7,6},{8,9},{9,8},{10,11... | collective-permute-start | bytes 393224 | tf_op jit(solution)/shard_map/ppermute | solution.py:608
  60.7 10.3 %collective-permute-start.14 = (bf16[2,128,256]{2,1,0:T(8,128)(2,1)S(1)}, bf16[2,128,256]{2,1,0:T(8,128)(2,1)S(1)}, u32[]{:S(2)}, u32[]{:S(2)}) collective-permute-start(bf16[2,128,256]{2,1,0:T(8,128)(2,1)S(1)} %collective-permute-done.6.refs_6_), channel_id=1, source_target_pairs={{0,1},{1,0},{2,3},{3,2},{4,5},{5,4},{6,7},{7,6},{8,9},{9,8},{10,11... | collective-permute-start | bytes 393224 | tf_op jit(solution)/shard_map/ppermute | solution.py:608
  61.2 9.9 %collective-permute-start.15 = (bf16[2,128,256]{2,1,0:T(8,128)(2,1)S(1)}, bf16[2,128,256]{2,1,0:T(8,128)(2,1)S(1)}, u32[]{:S(2)}, u32[]{:S(2)}) collective-permute-start(bf16[2,128,256]{2,1,0:T(8,128)(2,1)S(1)} %collective-permute-done.7.refs_7_), channel_id=1, source_target_pairs={{0,1},{1,0},{2,3},{3,2},{4,5},{5,4},{6,7},{7,6},{8,9},{9,8},{10,11... | collective-permute-start | bytes 393224 | tf_op jit(solution)/shard_map/ppermute | solution.py:608
  61.3 9.8 %collective-permute-start.10 = (bf16[2,128,256]{2,1,0:T(8,128)(2,1)S(1)}, bf16[2,128,256]{2,1,0:T(8,128)(2,1)S(1)}, u32[]{:S(2)}, u32[]{:S(2)}) collective-permute-start(bf16[2,128,256]{2,1,0:T(8,128)(2,1)S(1)} %collective-permute-done.2.refs_2_), channel_id=1, source_target_pairs={{0,1},{1,0},{2,3},{3,2},{4,5},{5,4},{6,7},{7,6},{8,9},{9,8},{10,11... | collective-permute-start | bytes 393224 | tf_op jit(solution)/shard_map/ppermute | solution.py:608
  61.7 14.6 %copy-start.1 = (f32[256]{0:T(256)S(1)}, f32[256]{0:T(256)}, u32[]{:S(2)}) copy-start(f32[256]{0:T(256)} %param.18) | copy-start | bytes 3076
  71.1 5.2 %copy-start.12 = (bf16[2,128,256]{2,1,0:T(8,128)(2,1)}, bf16[2,128,256]{2,1,0:T(8,128)(2,1)S(1)}, u32[]{:S(2)}) copy-start(bf16[2,128,256]{2,1,0:T(8,128)(2,1)S(1)} %collective-permute-done.15.refs_15_) | copy-start | bytes 393220
  87.3 55.3 %all-to-all-start.1 = ((bf16[32,128,256]{2,1,0:T(8,128)(2,1)}), bf16[32,128,256]{2,1,0:T(8,128)(2,1)}, u32[]{:S(2)}, u32[]{:S(2)}) async-start(bf16[32,128,256]{2,1,0:T(8,128)(2,1)} %get-tuple-element.50), calls=%async_computation.1 | async-start | bytes 4194304 | tf_op jit(solution)/shard_map/all_to_all | solution.py:564
  100.7 24.9 %copy-start.10 = (s32[1,32,128]{2,1,0:T(8,128)S(1)}, s32[1,32,128]{2,1,0:T(8,128)}, u32[]{:S(2)}) copy-start(s32[1,32,128]{2,1,0:T(8,128)} %param.11) | copy-start | bytes 49156
  100.7 24.9 %copy-start.11 = (s32[1,32]{1,0:T(1,128)S(1)}, s32[1,32]{1,0:T(1,128)}, u32[]{:S(2)}) copy-start(s32[1,32]{1,0:T(1,128)} %counts_in.5) | copy-start | bytes 388
  100.7 30.8 %copy-start = (bf16[256,256]{1,0:T(8,128)(2,1)S(1)}, bf16[256,256]{1,0:T(8,128)(2,1)}, u32[]{:S(2)}) copy-start(bf16[256,256]{1,0:T(8,128)(2,1)} %w_self.3) | copy-start | bytes 393220
  100.7 30.8 %copy-start.5 = (bf16[4096,256]{1,0:T(8,128)(2,1)S(1)}, bf16[4096,256]{1,0:T(8,128)(2,1)}, u32[]{:S(2)}) copy-start(bf16[4096,256]{1,0:T(8,128)(2,1)} %get-tuple-element.48.dpre_b) | copy-start | bytes 6291460
  102.7 1.9 %collective-permute-start.16 = (f32[288,256]{1,0:T(8,128)}, f32[288,256]{1,0:T(8,128)}, u32[]{:S(2)}, u32[]{:S(2)}) collective-permute-start(f32[288,256]{1,0:T(8,128)} %slice_select_fusion), channel_id=1, source_target_pairs={{0,1},{1,0},{2,3},{3,2},{4,5},{5,4},{6,7},{7,6},{8,9},{9,8},{10,11... | collective-permute-start | bytes 884744 | tf_op jit(solution)/shard_map/ppermute | solution.py:608
  108.2 8.2 %collective-permute-start.17 = (f32[144,256]{1,0:T(8,128)}, f32[144,256]{1,0:T(8,128)S(1)}, u32[]{:S(2)}, u32[]{:S(2)}) collective-permute-start(f32[144,256]{1,0:T(8,128)} %slice_select_fusion.1), channel_id=1, source_target_pairs={{0,8},{1,9},{2,10},{3,11},{4,12},{5,13},{6,14},{7,15},{8,0},{9,1},... | collective-permute-start | bytes 442376 | tf_op jit(solution)/shard_map/ppermute | solution.py:608
  117.3 5.7 %collective-permute-start.18 = (f32[72,256]{1,0:T(8,128)S(1)}, f32[72,256]{1,0:T(8,128)S(1)}, u32[]{:S(2)}, u32[]{:S(2)}) collective-permute-start(f32[72,256]{1,0:T(8,128)S(1)} %slice_select_fusion.2), channel_id=1, source_target_pairs={{0,16},{1,17},{2,18},{3,19},{4,20},{5,21},{6,22},{7,23},{8,24},{9,... | collective-permute-start | bytes 221192 | tf_op jit(solution)/shard_map/ppermute | solution.py:608
  123.1 5.4 %collective-permute-start.19 = (f32[72,256]{1,0:T(8,128)S(1)}, f32[72,256]{1,0:T(8,128)S(1)}, u32[]{:S(2)}, u32[]{:S(2)}) collective-permute-start(f32[72,256]{1,0:T(8,128)S(1)} %select_add_fusion.2), channel_id=1, source_target_pairs={{0,2},{1,3},{2,0},{3,1},{4,6},{5,7},{6,4},{7,5},{8,10},{9,11},{10,... | collective-permute-start | bytes 221192 | tf_op jit(solution)/shard_map/ppermute | solution.py:608
  128.5 14.0 %collective-permute-start.20 = (f32[72,256]{1,0:T(8,128)S(1)}, f32[72,256]{1,0:T(8,128)S(1)}, u32[]{:S(2)}, u32[]{:S(2)}) collective-permute-start(f32[72,256]{1,0:T(8,128)S(1)} %add.22), channel_id=1, source_target_pairs={{0,4},{1,5},{2,6},{3,7},{4,0},{5,1},{6,2},{7,3},{8,12},{9,13},{10,... | collective-permute-start | bytes 221192 | tf_op jit(solution)/shard_map/ppermute | solution.py:608
  143.4 13.6 %all-to-all-start.2 = ((f32[8,72,256]{2,1,0:T(8,128)}), f32[8,72,256]{2,1,0:T(8,128)S(1)}, u32[]{:S(2)}, u32[]{:S(2)}) async-start(f32[8,72,256]{2,1,0:T(8,128)} %broadcast_in_dim.17), calls=%async_computation.2 | async-start | bytes 1179648 | tf_op jit(solution)/shard_map/all_to_all | solution.py:564
  (5 other events, 6.5 us)
